TPU v7x, 256 devices: a whole 4x4x8 slice. The times are simulated.
256 devices in a mesh: row: 32 (over y, z), col: 8 (over x, core).
Axes of the slice: x: 4, y: 4, z: 8, core: 2. Of those that a mesh axis runs over, the one named last changes fastest.
Arguments:
- eigvec: float32 [8, 32, 128, 2048], P(None, 'row', None, 'col'), may hold values from -6 to 6
- reflectors: float32 [2, 8, 32, 256, 128], P(None, None, 'row', 'col'), may hold values from -6 to 6
- sweep_group: int32 [2, 8, 32], P(None, None, 'row'), may hold values from -1 to 254, as said below
Outputs:
- transformed: float32 [8, 32, 128, 2048], P(None, 'row', None, 'col')
Inputs may be any that keep to these rules, and one draw needn't show every extreme that they name: `sweep_group`: -1 where no diamond sits at that diagonal and tile position (tile position l * R + r for entry [d, l, r]); otherwise the diamond's sweep group, at most its tile position. Within one diagonal no two diamonds sit at adjacent tile positions, and none sits at the last tile position 255.
All inputs are finite; a program needn't handle non-finite values.
Results may differ from a plain program's by a relative error of at most 0.0003.
Values sent between devices are 32-bit elements.
A program may use at most 128 MiB of HBM per device.

v0:
```python
import jax
import jax.numpy as jnp
from jax import lax
from jax.experimental import pallas as pl
from jax.experimental.pallas import tpu as pltpu
from jax.sharding import PartitionSpec as P

MESH = pl.DeviceIdType.MESH
f32, bf16 = jnp.float32, jnp.bfloat16


def split(a):
    hi = a.astype(bf16)
    return hi, (a - hi.astype(f32)).astype(bf16)


def mm(a, b):
    return jnp.dot(a, b, preferred_element_type=f32)


def square_dot(a, b):
    n = a.shape[-1]
    a_hi, a_lo = split(a)
    b_hi, b_lo = split(b)
    right = jnp.concatenate([b_hi, b_lo], axis=1)
    both = mm(jnp.concatenate([a_hi, a_lo], axis=1), jnp.concatenate([right, right], axis=0))
    return both[:, :n] + both[:, n:]


def factor_panels(panels):
    depth, band = panels[0].shape
    rows = lax.broadcasted_iota(jnp.int32, (depth, band), 0)
    cols = lax.broadcasted_iota(jnp.int32, (depth, band), 1)
    inside = (rows >= cols + 1) & (rows <= cols + band)
    leading = rows == cols + 1
    r = lax.broadcasted_iota(jnp.int32, (band, band), 0)
    c = lax.broadcasted_iota(jnp.int32, (band, band), 1)
    eye, above = r == c, r < c
    halves, turned, factors, inverses = [], [], [], []
    for panel in panels:
        vectors = jnp.where(leading, 1.0, jnp.where(inside, panel, 0.0))
        v_hi, v_lo = split(vectors)
        t_hi, t_lo = split(vectors.T)
        both = mm(t_hi, jnp.concatenate([v_hi, v_lo], axis=1))
        gram = both[:, :band] + both[:, band:] + mm(t_lo, v_hi)
        on_diagonal = jnp.where(eye, gram, 0.0)
        along = 2.0 / jnp.sum(on_diagonal, axis=0, keepdims=True)
        down = 2.0 / jnp.sum(on_diagonal, axis=1, keepdims=True)
        pair = above & (r // 2 == c // 2)
        inverse = jnp.where(eye, along, 0.0) - jnp.where(pair, gram * along * down, 0.0)
        halves.append((v_hi, v_lo))
        turned.append((t_hi, t_lo))
        factors.append(gram)
        inverses.append(inverse)
    block = 2
    while block < band:
        coupling = above & (r // block != c // block) & (r // (2 * block) == c // (2 * block))
        middles = [square_dot(jnp.where(coupling, f, 0.0), x) for f, x in zip(factors, inverses)]
        inverses = [x - square_dot(x, m) for x, m in zip(inverses, middles)]
        block *= 2
    results = []
    for (v_hi, v_lo), (t_hi, t_lo), inverse in zip(halves, turned, inverses):
        i_hi, i_lo = split(inverse)
        solver = mm(jnp.concatenate([i_hi, i_lo], axis=1), jnp.concatenate([t_hi, t_hi], axis=0)) + mm(i_hi, t_lo)
        p_hi, p_lo = split(solver)
        results.append((v_hi, v_lo, p_hi, p_lo))
    return results


def kernel(n_row, n_x, eig, refl, flags, out,
           xin, xb, xs, xf, xq, xc, u1, us, u2, s1, ss, s2, d1, ds, d2, pan, vv, pp,
           in_sem, pan_in, pan_send, pan_recv, rel_send, rel_recv,
           up_send, up_recv, dn_send, dn_recv, out_sem):
    row = lax.axis_index("row")
    col = lax.axis_index("col")
    band = xin.shape[1]
    per = pan.shape[2]
    x, core = col // 2, lax.rem(col, 2)
    first = row == 0
    last = row == n_row - 1
    shift = jnp.where(first, 1, 0)
    above = lax.rem(row + n_row - 1, n_row)
    below = lax.rem(row + 1, n_row)
    twice0 = jnp.where(lax.rem(row, 2) == 1, 0, per)
    once0 = per - twice0
    partner = x * 2 + (1 - core)
    peers = [lax.rem(x + k, n_x) * 2 + core for k in range(1, n_x)]

    chunk_of = ((0, twice0), (0, once0), (1, once0), (1, twice0))
    tiles_in = pltpu.make_async_copy(eig.at[:, 0], xin, in_sem)
    tiles_in.start()
    panels_in = []
    for k, (d, l0) in enumerate(chunk_of):
        copy = pltpu.make_async_copy(refl.at[d, pl.ds(l0, per), 0], pan.at[k, col], pan_in.at[k])
        copy.start()
        panels_in.append(copy)

    barrier = pltpu.get_barrier_semaphore()
    for r_, c_ in [(above, col), (below, col), (row, partner)] + [(row, p) for p in peers]:
        pl.semaphore_signal(barrier, inc=1, device_id=(r_, c_), device_id_type=MESH)
    pl.semaphore_wait(barrier, 3 + len(peers))

    def remote(src, dst, ssem, rsem, r_, c_):
        return pltpu.make_async_remote_copy(src_ref=src, dst_ref=dst, send_sem=ssem, recv_sem=rsem,
                                            device_id=(r_, c_), device_id_type=MESH)

    def upward(kind, src, dst, i):
        return remote(src, dst.at[i], up_send.at[kind, i], up_recv.at[kind, i], above, col)

    def downward(kind, src, dst, i):
        return remote(src, dst.at[i], dn_send.at[kind, i], dn_recv.at[kind, i], below, col)

    def share(k, j):
        return remote(pan.at[k, col], pan.at[k, col], pan_send.at[k, j], pan_recv.at[k, j],
                      row, partner if j == n_x - 1 else peers[j])

    def came(k, j):
        origin = partner if j == n_x - 1 else lax.rem(x + n_x - 1 - j, n_x) * 2 + core
        return remote(pan.at[k, origin], pan.at[k, origin], pan_send.at[k, j], pan_recv.at[k, j], row, partner)

    def passed(k, j):
        origin = lax.rem(x + n_x - 1 - j, n_x) * 2 + core
        return remote(pan.at[k, origin], pan.at[k, origin], rel_send.at[k, j], rel_recv.at[k, j], row, partner)

    def passed_here(k, j):
        origin = lax.rem(x + n_x - 1 - j, n_x) * 2 + (1 - core)
        return remote(pan.at[k, origin], pan.at[k, origin], rel_send.at[k, j], rel_recv.at[k, j], row, partner)

    order = [0, n_x - 2] + list(range(1, n_x - 2))
    panels_in[0].wait()
    for j in order + [n_x - 1]:
        share(0, j).start()
    tiles_in.wait()
    for i in range(per):
        upward(0, xin.at[once0 + i + shift], u1, i).start()
    for k in range(1, 4):
        panels_in[k].wait()
        for j in order + [n_x - 1]:
            share(k, j).start()

    def pass_on(k):
        for j in order:
            came(k, j).wait_recv()
            passed(k, j).start()

    def settle(k):
        came(k, n_x - 1).wait_recv()
        for j in order:
            passed_here(k, j).wait_recv()

    def factor_chunk(k):
        raw = [pan[k, :, i].reshape(2 * band, band) for i in range(per)]
        for i, (v_hi, v_lo, p_hi, p_lo) in enumerate(factor_panels(raw)):
            vv[k, i, 0] = v_hi
            vv[k, i, 1] = v_lo
            pp[k, i, 0] = p_hi
            pp[k, i, 1] = p_lo

    def apply(k, i, d, l, upper, lower):
        s_hi, s_lo = split(jnp.concatenate([upper, lower], axis=0))
        p_hi, p_lo = pp[k, i, 0], pp[k, i, 1]
        v_hi, v_lo = vv[k, i, 0], vv[k, i, 1]
        w_hi, w_lo = split(mm(p_hi, s_hi) + mm(p_hi, s_lo) + mm(p_lo, s_hi))
        change = mm(jnp.concatenate([v_hi, v_lo], axis=1), jnp.concatenate([w_hi, w_hi], axis=0)) + mm(v_hi, w_lo)
        active = flags[d, l, 0] >= 0
        return (jnp.where(active, upper - change[:band], upper), jnp.where(active, lower - change[band:], lower))

    pass_on(0)
    settle(0)
    factor_chunk(0)
    pass_on(1)

    def early(i, carry):
        l = twice0 + i
        upward(0, u1.at[i], u1, i).wait_recv()
        upper, lower = apply(0, i, 0, l, xin[l], u1[i])
        s1[i] = lower
        xb[i] = upper
        downward(0, s1.at[i], d1, i).start()

        @pl.when(jnp.logical_not(first))
        def _():
            upward(1, xb.at[i], us, i).start()

        @pl.when(first & (i > 0))
        def _():
            upward(1, xb.at[i], us, i - 1).start()

        return carry

    lax.fori_loop(0, per, early, 0)

    @pl.when(first)
    def _():
        upward(1, xb.at[per - 1], us, per - 1).start()

    settle(1)
    pass_on(2)
    factor_chunk(1)
    settle(2)
    pass_on(3)
    factor_chunk(2)

    def middle(i, carry):
        l = once0 + i

        @pl.when(first & (i == 0))
        def _():
            xq[...] = xin[once0]

        @pl.when(jnp.logical_not(first & (i == 0)))
        def _():
            j = i - shift
            downward(0, d1.at[j], d1, j).wait_recv()
            xq[...] = d1[j]

        upward(1, us.at[i], us, i).wait_recv()
        upper, lower = apply(1, i, 0, l, xq[...], us[i])
        upper, lower = apply(2, i, 1, l, upper, lower)
        ss[i] = lower
        xs[i] = upper
        downward(1, ss.at[i], ds, i).start()

        @pl.when(jnp.logical_not(first & (i == 0)))
        def _():
            upward(2, xs.at[i], u2, i - shift).start()

        return carry

    lax.fori_loop(0, per, middle, 0)
    settle(3)
    factor_chunk(3)

    @pl.when(first)
    def _():
        downward(0, d1.at[per - 1], d1, per - 1).wait_recv()
        xq[...] = jnp.where(flags[0, twice0, 0] >= 0, xb[0], d1[per - 1])
        upward(2, xq, u2, per - 1).start()

    def late(i, carry):
        l = twice0 + i

        @pl.when(jnp.logical_not(first & (i == 0)))
        def _():
            j = i - shift
            downward(1, ds.at[j], ds, j).wait_recv()

            xc[...] = ds[j]

        @pl.when(first & (i == 0))
        def _():
            xc[...] = xq[...]
            downward(1, ds.at[per - 1], ds, per - 1).wait_recv()

        upward(2, u2.at[i], u2, i).wait_recv()
        upper, lower = apply(3, i, 1, l, xc[...], u2[i])
        s2[i] = lower
        xf[i] = upper
        downward(2, s2.at[i], d2, i).start()

        @pl.when(jnp.logical_not(first & (i == 0)))
        def _():
            pltpu.make_async_copy(xf.at[i], out.at[l, 0], out_sem.at[i]).start()

        return carry

    lax.fori_loop(0, per, late, 0)

    def close(i, carry):
        @pl.when(jnp.logical_not(first & (i == 0)))
        def _():
            j = i - shift
            downward(2, d2.at[j], d2, j).wait_recv()
            pltpu.make_async_copy(d2.at[j], out.at[once0 + i, 0], out_sem.at[per + i]).start()

        @pl.when(first & (i == 0))
        def _():
            pltpu.make_async_copy(xs.at[i], out.at[once0 + i, 0], out_sem.at[per + i]).start()

        return carry

    lax.fori_loop(0, per, close, 0)

    @pl.when(first)
    def _():
        downward(2, d2.at[per - 1], d2, per - 1).wait_recv()
        xq2 = jnp.where(flags[1, twice0, 0] >= 0, xf[0], d2[per - 1])
        xb[0] = xq2
        pltpu.make_async_copy(xb.at[0], out.at[twice0, 0], out_sem.at[0]).start()

    def drain(i, carry):
        for kind in range(3):
            upward(kind, xb.at[i], u1, i).wait_send()
            downward(kind, xb.at[i], d1, i).wait_send()
        pltpu.make_async_copy(xf.at[i], out.at[twice0 + i, 0], out_sem.at[i]).wait()
        pltpu.make_async_copy(xf.at[i], out.at[once0 + i, 0], out_sem.at[per + i]).wait()
        for j in range(n_x):
            share(i, j).wait_send()
        for j in range(n_x - 1):
            passed(i, j).wait_send()
        return carry

    lax.fori_loop(0, 4, drain, 0)


def local(n_row, n_x, eigvec, reflectors, sweep_group):
    tiles, _, band, width = eigvec.shape
    rows = reflectors.shape[3]
    per = tiles // 2
    tile = pltpu.VMEM((per, band, width), f32)
    dma = pltpu.SemaphoreType.DMA
    import functools
    return pl.pallas_call(
        functools.partial(kernel, n_row, n_x),
        out_shape=jax.ShapeDtypeStruct(eigvec.shape, f32),
        in_specs=[pl.BlockSpec(memory_space=pl.ANY), pl.BlockSpec(memory_space=pl.ANY),
                  pl.BlockSpec(memory_space=pltpu.SMEM)],
        out_specs=pl.BlockSpec(memory_space=pl.ANY),
        scratch_shapes=[
            pltpu.VMEM((tiles, band, width), f32),
            tile, tile, tile, pltpu.VMEM((band, width), f32), pltpu.VMEM((band, width), f32),
            tile, tile, tile, tile, tile, tile, tile, tile, tile,
            pltpu.VMEM((4, 2 * n_x, per, rows, band), f32),
            pltpu.VMEM((4, per, 2, 2 * band, band), bf16),
            pltpu.VMEM((4, per, 2, band, 2 * band), bf16),
            dma, dma((4,)), dma((4, n_x)), dma((4, n_x)), dma((4, n_x - 1)), dma((4, n_x - 1)),
            dma((3, per)), dma((3, per)), dma((3, per)), dma((3, per)), dma((2 * per,)),
        ],
        compiler_params=pltpu.CompilerParams(
            collective_id=0, has_side_effects=True, vmem_limit_bytes=48 * 1024 * 1024),
    )(eigvec, reflectors, sweep_group)


def solution(mesh):
    import functools
    return jax.shard_map(
        functools.partial(local, mesh.shape["row"], mesh.shape["col"] // 2),
        mesh=mesh,
        in_specs=(
            P(None, "row", None, "col"),
            P(None, None, "row", "col", None),
            P(None, None, "row"),
        ),
        out_specs=P(None, "row", None, "col"),
        check_vma=False,
    )
```

profile of v0, /device:TPU:1, one launch (start us, length us, event | category | flops | bytes accessed | tf_op | source)
XLA Modules:
  0.0 62.4 jit_solution(8387379157965575492)
XLA Ops:
  0.0 0.8 %copy.4.flags = s32[2,8,1]{2,1,0:T(8,128)S(1)} copy(s32[2,8,1]{1,2,0:T(1,128)} %param.5) | data formatting | bytes 128 | tf_op args[2]
  0.8 0.0 copy-start
  0.8 1.2 %copy-done = f32[8,1,128,256]{3,2,1,0:T(8,128)S(1)} copy-done((f32[8,1,128,256]{3,2,1,0:T(8,128)S(1)}, f32[8,1,128,256]{3,2,1,0:T(8,128)}, u32[]{:S(2)}) %copy-start) | copy-done | bytes 1048600
  2.0 0.0 copy-start.1
  2.0 0.9 %copy-done.1 = f32[2,8,1,32,128]{4,3,2,1,0:T(8,128)S(1)} copy-done((f32[2,8,1,32,128]{4,3,2,1,0:T(8,128)S(1)}, f32[2,8,1,32,128]{4,3,2,1,0:T(8,128)}, u32[]{:S(2)}) %copy-start.1) | copy-done | bytes 262168
  2.9 58.5 %shard_map.37 = f32[8,1,128,256]{3,2,1,0:T(8,128)S(1)} custom-call(f32[8,1,128,256]{3,2,1,0:T(8,128)S(1)} %copy-done, f32[2,8,1,32,128]{4,3,2,1,0:T(8,128)S(1)} %copy-done.1, s32[2,8,1]{2,1,0:T(8,128)S(1)} %copy.4.flags), custom_call_target="tpu_custom_call" | custom-call | tf_op jit(solution)/shard_map/pallas_call | solution.py:313
  61.5 1.0 %copy.6 = f32[8,1,128,256]{3,2,1,0:T(8,128)} copy(f32[8,1,128,256]{3,2,1,0:T(8,128)S(1)} %shard_map.37) | data formatting | bytes 2097152
Async XLA Ops:
  0.8 1.2 %copy-start = (f32[8,1,128,256]{3,2,1,0:T(8,128)S(1)}, f32[8,1,128,256]{3,2,1,0:T(8,128)}, u32[]{:S(2)}) copy-start(f32[8,1,128,256]{3,2,1,0:T(8,128)} %eig.1) | copy-start | bytes 3145732
  2.0 0.9 %copy-start.1 = (f32[2,8,1,32,128]{4,3,2,1,0:T(8,128)S(1)}, f32[2,8,1,32,128]{4,3,2,1,0:T(8,128)}, u32[]{:S(2)}) copy-start(f32[2,8,1,32,128]{4,3,2,1,0:T(8,128)} %refl.1) | copy-start | bytes 786436
where the time goes:
time: 63 us; the launch traced here: 62.4 us
  Pallas kernels  58.5 us (93%)
  local copies, waits for them, and re-layouts  3.9 us (6%)
    pallas_call x1, Pallas kernels, local(): pl.pallas_call(functools.partial(kernel, n_row, n_x), out_shape=jax.Shape...  58.5 us
    unnamed x6, local copies, waits for them, and re-layouts  3.9 us

commit v1 on v0

--- a/solution.py
+++ b/solution.py
@@ -1,3 +1,5 @@
+import functools
+
 import jax
 import jax.numpy as jnp
 from jax import lax
@@ -67,9 +69,9 @@
     return results
 
 
-def kernel(n_row, n_x, eig, refl, flags, out,
-           xin, xb, xs, xf, xq, xc, u1, us, u2, s1, ss, s2, d1, ds, d2, pan, vv, pp,
-           in_sem, pan_in, pan_send, pan_recv, rel_send, rel_recv,
+def kernel(n_row, n_x, eig, refl, flags_in, out,
+           flags, xin, xb, xs, xf, xq, xc, u1, us, u2, s1, ss, s2, d1, ds, d2, pan, vv, pp,
+           flag_sem, in_sem, pan_in, pan_send, pan_recv, rel_send, rel_recv,
            up_send, up_recv, dn_send, dn_recv, out_sem):
     row = lax.axis_index("row")
     col = lax.axis_index("col")
@@ -89,6 +91,8 @@
     chunk_of = ((0, twice0), (0, once0), (1, once0), (1, twice0))
     tiles_in = pltpu.make_async_copy(eig.at[:, 0], xin, in_sem)
     tiles_in.start()
+    flags_copy = pltpu.make_async_copy(flags_in, flags, flag_sem)
+    flags_copy.start()
     panels_in = []
     for k, (d, l0) in enumerate(chunk_of):
         copy = pltpu.make_async_copy(refl.at[d, pl.ds(l0, per), 0], pan.at[k, col], pan_in.at[k])
@@ -109,6 +113,11 @@
 
     def downward(kind, src, dst, i):
         return remote(src, dst.at[i], dn_send.at[kind, i], dn_recv.at[kind, i], below, col)
+
+    next_shift = jnp.where(last, 1, 0)
+
+    def home(i, src):
+        return remote(src, out.at[twice0 + next_shift + i, 0], dn_send.at[2, i], dn_recv.at[2, i], below, col)
 
     def share(k, j):
         return remote(pan.at[k, col], pan.at[k, col], pan_send.at[k, j], pan_recv.at[k, j],
@@ -148,9 +157,10 @@
         for j in order:
             passed_here(k, j).wait_recv()
 
-    def factor_chunk(k):
-        raw = [pan[k, :, i].reshape(2 * band, band) for i in range(per)]
-        for i, (v_hi, v_lo, p_hi, p_lo) in enumerate(factor_panels(raw)):
+    def factor_chunks(*ks):
+        at = [(k, i) for k in ks for i in range(per)]
+        raw = [pan[k, :, i].reshape(2 * band, band) for k, i in at]
+        for (k, i), (v_hi, v_lo, p_hi, p_lo) in zip(at, factor_panels(raw)):
             vv[k, i, 0] = v_hi
             vv[k, i, 1] = v_lo
             pp[k, i, 0] = p_hi
@@ -162,12 +172,13 @@
         v_hi, v_lo = vv[k, i, 0], vv[k, i, 1]
         w_hi, w_lo = split(mm(p_hi, s_hi) + mm(p_hi, s_lo) + mm(p_lo, s_hi))
         change = mm(jnp.concatenate([v_hi, v_lo], axis=1), jnp.concatenate([w_hi, w_hi], axis=0)) + mm(v_hi, w_lo)
-        active = flags[d, l, 0] >= 0
+        active = flags[d, l] >= 0
         return (jnp.where(active, upper - change[:band], upper), jnp.where(active, lower - change[band:], lower))
 
     pass_on(0)
     settle(0)
-    factor_chunk(0)
+    flags_copy.wait()
+    factor_chunks(0)
     pass_on(1)
 
     def early(i, carry):
@@ -188,18 +199,18 @@
 
         return carry
 
-    lax.fori_loop(0, per, early, 0)
+    lax.fori_loop(0, per - 1, early, 0)
+    pass_on(2)
+    settle(1)
+    settle(2)
+    factor_chunks(1, 2)
+    lax.fori_loop(per - 1, per, early, 0)
 
     @pl.when(first)
     def _():
         upward(1, xb.at[per - 1], us, per - 1).start()
 
-    settle(1)
-    pass_on(2)
-    factor_chunk(1)
-    settle(2)
     pass_on(3)
-    factor_chunk(2)
 
     def middle(i, carry):
         l = once0 + i
@@ -227,14 +238,15 @@
 
         return carry
 
-    lax.fori_loop(0, per, middle, 0)
+    lax.fori_loop(0, 1, middle, 0)
     settle(3)
-    factor_chunk(3)
+    factor_chunks(3)
+    lax.fori_loop(1, per, middle, 0)
 
     @pl.when(first)
     def _():
         downward(0, d1.at[per - 1], d1, per - 1).wait_recv()
-        xq[...] = jnp.where(flags[0, twice0, 0] >= 0, xb[0], d1[per - 1])
+        xq[...] = jnp.where(flags[0, twice0] >= 0, xb[0], d1[per - 1])
         upward(2, xq, u2, per - 1).start()
 
     def late(i, carry):
@@ -256,7 +268,14 @@
         upper, lower = apply(3, i, 1, l, xc[...], u2[i])
         s2[i] = lower
         xf[i] = upper
-        downward(2, s2.at[i], d2, i).start()
+        @pl.when(last & (i == per - 1))
+        def _():
+            remote(s2.at[i], d2, dn_send.at[2, i], dn_recv.at[2, i], below, col).start()
+
+        @pl.when(jnp.logical_not(last & (i == per - 1)))
+        def _():
+            home(i, s2.at[i]).start()
+
 
         @pl.when(jnp.logical_not(first & (i == 0)))
         def _():
@@ -270,12 +289,7 @@
         @pl.when(jnp.logical_not(first & (i == 0)))
         def _():
             j = i - shift
-            downward(2, d2.at[j], d2, j).wait_recv()
-            pltpu.make_async_copy(d2.at[j], out.at[once0 + i, 0], out_sem.at[per + i]).start()
-
-        @pl.when(first & (i == 0))
-        def _():
-            pltpu.make_async_copy(xs.at[i], out.at[once0 + i, 0], out_sem.at[per + i]).start()
+            remote(s2.at[j], out.at[once0 + i, 0], dn_send.at[2, j], dn_recv.at[2, j], below, col).wait_recv()
 
         return carry
 
@@ -283,17 +297,17 @@
 
     @pl.when(first)
     def _():
-        downward(2, d2.at[per - 1], d2, per - 1).wait_recv()
-        xq2 = jnp.where(flags[1, twice0, 0] >= 0, xf[0], d2[per - 1])
-        xb[0] = xq2
+        pltpu.make_async_copy(xs.at[0], out.at[once0, 0], out_sem.at[per]).start()
+        remote(xq, d2, dn_send.at[2, per - 1], dn_recv.at[2, per - 1], below, col).wait_recv()
+        xb[0] = jnp.where(flags[1, twice0] >= 0, xf[0], d2[...])
         pltpu.make_async_copy(xb.at[0], out.at[twice0, 0], out_sem.at[0]).start()
+        pltpu.make_async_copy(xs.at[0], out.at[once0, 0], out_sem.at[per]).wait()
 
     def drain(i, carry):
         for kind in range(3):
             upward(kind, xb.at[i], u1, i).wait_send()
             downward(kind, xb.at[i], d1, i).wait_send()
         pltpu.make_async_copy(xf.at[i], out.at[twice0 + i, 0], out_sem.at[i]).wait()
-        pltpu.make_async_copy(xf.at[i], out.at[once0 + i, 0], out_sem.at[per + i]).wait()
         for j in range(n_x):
             share(i, j).wait_send()
         for j in range(n_x - 1):
@@ -309,30 +323,29 @@
     per = tiles // 2
     tile = pltpu.VMEM((per, band, width), f32)
     dma = pltpu.SemaphoreType.DMA
-    import functools
+    hbm = lambda array: pltpu.with_memory_space_constraint(array, pltpu.HBM)
     return pl.pallas_call(
         functools.partial(kernel, n_row, n_x),
         out_shape=jax.ShapeDtypeStruct(eigvec.shape, f32),
-        in_specs=[pl.BlockSpec(memory_space=pl.ANY), pl.BlockSpec(memory_space=pl.ANY),
-                  pl.BlockSpec(memory_space=pltpu.SMEM)],
+        in_specs=[pl.BlockSpec(memory_space=pltpu.HBM)] * 3,
         out_specs=pl.BlockSpec(memory_space=pl.ANY),
         scratch_shapes=[
+            pltpu.SMEM(sweep_group.shape[:2], jnp.int32),
             pltpu.VMEM((tiles, band, width), f32),
             tile, tile, tile, pltpu.VMEM((band, width), f32), pltpu.VMEM((band, width), f32),
-            tile, tile, tile, tile, tile, tile, tile, tile, tile,
+            tile, tile, tile, tile, tile, tile, tile, tile, pltpu.VMEM((band, width), f32),
             pltpu.VMEM((4, 2 * n_x, per, rows, band), f32),
             pltpu.VMEM((4, per, 2, 2 * band, band), bf16),
             pltpu.VMEM((4, per, 2, band, 2 * band), bf16),
-            dma, dma((4,)), dma((4, n_x)), dma((4, n_x)), dma((4, n_x - 1)), dma((4, n_x - 1)),
-            dma((3, per)), dma((3, per)), dma((3, per)), dma((3, per)), dma((2 * per,)),
+            dma, dma, dma((4,)), dma((4, n_x)), dma((4, n_x)), dma((4, n_x - 1)), dma((4, n_x - 1)),
+            dma((3, per)), dma((3, per)), dma((3, per)), dma((3, per)), dma((per + 1,)),
         ],
         compiler_params=pltpu.CompilerParams(
             collective_id=0, has_side_effects=True, vmem_limit_bytes=48 * 1024 * 1024),
-    )(eigvec, reflectors, sweep_group)
+    )(hbm(eigvec), hbm(reflectors), hbm(sweep_group.reshape(sweep_group.shape[:2])))
 
 
 def solution(mesh):
-    import functools
     return jax.shard_map(
         functools.partial(local, mesh.shape["row"], mesh.shape["col"] // 2),
         mesh=mesh,

time: 63 us -> 60.2 us (0.956)
  local copies, waits for them, and re-layouts: 3.9 us -> 0.97 us
    unnamed x6 -> x1, local copies, waits for them, and re-layouts: 3.9 us -> 0.97 us
where the time goes in v1:
time: 60.2 us; the launch traced here: 60.1 us
  Pallas kernels  59.1 us (98%)
  local copies, waits for them, and re-layouts  0.97 us (2%)
    pallas_call x1, Pallas kernels, local(): pl.pallas_call(functools.partial(kernel, n_row, n_x), out_shape=jax.Shape...  59.1 us

profile of v1, /device:TPU:1, one launch (start us, length us, event | category | flops | bytes accessed | tf_op | source)
XLA Modules:
  0.0 60.1 jit_solution(10979929587695898064)
XLA Ops:
  0.0 59.1 %shard_map.37 = f32[8,1,128,256]{3,2,1,0:T(8,128)S(1)} custom-call(f32[8,1,128,256]{3,2,1,0:T(8,128)} %eig.1, f32[2,8,1,32,128]{4,3,2,1,0:T(8,128)} %refl.1, s32[2,8]{1,0:T(2,128)} %bitcast.1), custom_call_target="tpu_custom_call" | custom-call | tf_op jit(solution)/shard_map/pallas_call | solution.py:327
  59.1 1.0 %copy.5 = f32[8,1,128,256]{3,2,1,0:T(8,128)} copy(f32[8,1,128,256]{3,2,1,0:T(8,128)S(1)} %shard_map.37) | data formatting | bytes 2097152

commit v2 on v1

v2 whole, which is shorter than its diff:
```python
import functools

import jax
import jax.numpy as jnp
from jax import lax
from jax.experimental import pallas as pl
from jax.experimental.pallas import tpu as pltpu
from jax.sharding import PartitionSpec as P

MESH = pl.DeviceIdType.MESH
f32, bf16 = jnp.float32, jnp.bfloat16
TILES, FEWER = 8, 3


def split(a):
    hi = a.astype(bf16)
    return hi, (a - hi.astype(f32)).astype(bf16)


def mm(a, b):
    return jnp.dot(a, b, preferred_element_type=f32)


def square_dot(a, b):
    n = a.shape[-1]
    a_hi, a_lo = split(a)
    b_hi, b_lo = split(b)
    right = jnp.concatenate([b_hi, b_lo], axis=1)
    both = mm(jnp.concatenate([a_hi, a_lo], axis=1), jnp.concatenate([right, right], axis=0))
    return both[:, :n] + both[:, n:]


def factor_panels(panels):
    depth, band = panels[0].shape
    rows = lax.broadcasted_iota(jnp.int32, (depth, band), 0)
    cols = lax.broadcasted_iota(jnp.int32, (depth, band), 1)
    inside = (rows >= cols + 1) & (rows <= cols + band)
    leading = rows == cols + 1
    r = lax.broadcasted_iota(jnp.int32, (band, band), 0)
    c = lax.broadcasted_iota(jnp.int32, (band, band), 1)
    eye, above, beside = r == c, r < c, (r + 1 == c) & (lax.rem(c, 2) == 1)
    halves, turned, factors, inverses = [], [], [], []
    coupled = above & (r // 2 != c // 2) & (r // 4 == c // 4)
    for panel in panels:
        vectors = jnp.where(leading, 1.0, jnp.where(inside, panel, 0.0))
        v_hi, v_lo = split(vectors)
        t_hi, t_lo = split(vectors.T)
        both = mm(t_hi, jnp.concatenate([v_hi, v_lo], axis=1))
        gram = both[:, :band] + both[:, band:] + mm(t_lo, v_hi)
        on_diagonal = jnp.where(eye, gram, 0.0)
        along = 2.0 / jnp.sum(on_diagonal, axis=0, keepdims=True)
        down = 2.0 / jnp.sum(on_diagonal, axis=1, keepdims=True)
        pair = jnp.where(beside, gram * along * down, 0.0)
        pair_along = -jnp.sum(pair, axis=0, keepdims=True)
        pair_down = -jnp.sum(pair, axis=1, keepdims=True)
        inverse = jnp.where(eye, along, 0.0) - pair
        upper_part = jnp.where(coupled, gram, 0.0)
        middle = upper_part * along + pltpu.roll(upper_part, 1, 1) * pair_along
        inverse = inverse - (middle * down + pltpu.roll(middle, band - 1, 0) * pair_down)
        halves.append((v_hi, v_lo))
        turned.append((t_hi, t_lo))
        factors.append(gram)
        inverses.append(inverse)
    block = 4
    while block < band:
        step = 4 if 4 * block <= band else 2
        coupling = above & (r // block != c // block) & (r // (step * block) == c // (step * block))
        if step == 2:
            middles = [square_dot(jnp.where(coupling, f, 0.0), x) for f, x in zip(factors, inverses)]
            inverses = [x - square_dot(x, m) for x, m in zip(inverses, middles)]
        else:
            moves = [square_dot(x, jnp.where(coupling, f, 0.0)) for f, x in zip(factors, inverses)]
            squares = [square_dot(m, m) for m in moves]
            firsts = [x - square_dot(m, x) for m, x in zip(moves, inverses)]
            inverses = [y + square_dot(q, y) for q, y in zip(squares, firsts)]
        block *= step
    results = []
    for (v_hi, v_lo), (t_hi, t_lo), inverse in zip(halves, turned, inverses):
        i_hi, i_lo = split(inverse)
        solver = mm(jnp.concatenate([i_hi, i_lo], axis=1), jnp.concatenate([t_hi, t_hi], axis=0)) + mm(i_hi, t_lo)
        p_hi, p_lo = split(solver)
        results.append((v_hi, v_lo, p_hi, p_lo))
    return results


def kernel(n_row, n_x, fewer, *refs):
    odd = lax.rem(lax.axis_index("row"), 2) == 1

    @pl.when(odd)
    def _():
        body(n_row, n_x, (0, fewer), (fewer, TILES - fewer), 0, *refs)

    @pl.when(jnp.logical_not(odd))
    def _():
        body(n_row, n_x, (fewer, TILES - fewer), (0, fewer), 1, *refs)


def body(n_row, n_x, twice, once, held, eig, refl, flags_in, out,
         flags, xin, xb, xs, xf, xq, xc, u1, us, u2, s1, ss, s2, d1, ds, d2, pan, vv, pp,
         flag_sem, in_sem, pan_in, pan_send, pan_recv, fwd_send, fwd_recv, rel_send, rel_recv,
         up_send, up_recv, dn_send, dn_recv, out_sem):
    row = lax.axis_index("row")
    col = lax.axis_index("col")
    band = xin.shape[1]
    x, core = col // 2, lax.rem(col, 2)
    first = row == 0
    last = row == n_row - 1
    shift = jnp.where(first, 1, 0)
    next_shift = jnp.where(last, 1, 0)
    above = lax.rem(row + n_row - 1, n_row)
    below = lax.rem(row + 1, n_row)
    (twice0, n_twice), (once0, n_once) = twice, once
    partner = x * 2 + (1 - core)
    x_right, x_left, x_far = lax.rem(x + 1, n_x), lax.rem(x + n_x - 1, n_x), lax.rem(x + 2, n_x)
    right, left = x_right * 2 + core, x_left * 2 + core

    chunks = ((0, *twice), (0, *once), (1, *once), (1, *twice))

    def shares(k, c, half=None):
        d, l0, n = chunks[k]
        lo, hi = {None: (0, n), 0: (0, n // 2), 1: (n // 2, n)}[half]
        return pan.at[d, pl.ds(l0 + lo, hi - lo), c]

    tiles_in = pltpu.make_async_copy(eig.at[:, 0], xin, in_sem)
    tiles_in.start()
    panels_in = []
    for k, (d, l0, n) in enumerate(chunks):
        copy = pltpu.make_async_copy(refl.at[d, pl.ds(l0, n), 0], shares(k, col), pan_in.at[k])
        copy.start()
        panels_in.append(copy)
    flags_copy = pltpu.make_async_copy(flags_in, flags, flag_sem)
    flags_copy.start()

    barrier = pltpu.get_barrier_semaphore()
    for r_, c_ in ((above, col), (below, col), (row, right), (row, left), (row, partner)):
        pl.semaphore_signal(barrier, inc=1, device_id=(r_, c_), device_id_type=MESH)
    pl.semaphore_wait(barrier, 5)

    def remote(src, dst, ssem, rsem, r_, c_):
        return pltpu.make_async_remote_copy(src_ref=src, dst_ref=dst, send_sem=ssem, recv_sem=rsem,
                                            device_id=(r_, c_), device_id_type=MESH)

    def upward(kind, src, dst, i):
        return remote(src, dst.at[i], up_send.at[kind, i], up_recv.at[kind, i], above, col)

    def downward(kind, src, dst, i):
        return remote(src, dst.at[i], dn_send.at[kind, i], dn_recv.at[kind, i], below, col)

    def home(i, src):
        return remote(src, out.at[twice0 + next_shift + i, 0], dn_send.at[2, i], dn_recv.at[2, i], below, col)

    def given(k, j):
        c = shares(k, col)
        return remote(c, c, pan_send.at[k, j], pan_recv.at[k, j], row, (right, left, partner)[j])

    def taken(k, j):
        c = shares(k, (left, right, partner)[j])
        return remote(c, c, pan_send.at[k, j], pan_recv.at[k, j], row, partner)

    def onward(k, j):
        c = shares(k, (left, right)[j], j)
        return remote(c, c, fwd_send.at[k, j], fwd_recv.at[k, j], row, (right, left)[j])

    def onward_taken(k, j):
        c = shares(k, x_far * 2 + core, j)
        return remote(c, c, fwd_send.at[k, j], fwd_recv.at[k, j], row, partner)

    def across(k, j, c_):
        origin = (x_left, x_right, x_far, x_far)[j] * 2 + c_
        c = shares(k, origin, None if j < 2 else j - 2)
        return remote(c, c, rel_send.at[k, j], rel_recv.at[k, j], row, partner)

    def give(k):
        panels_in[k].wait()
        for j in range(3):
            given(k, j).start()

    def near(k):
        for j in range(2):
            taken(k, j).wait_recv()
            onward(k, j).start()
            across(k, j, core).start()

    def far(k):
        for j in range(2):
            onward_taken(k, j).wait_recv()
            across(k, 2 + j, core).start()

    def settle(k):
        taken(k, 2).wait_recv()
        for j in range(4):
            across(k, j, 1 - core).wait_recv()

    def factor_chunks(*ks):
        at = [(chunks[k][0], chunks[k][1] + i) for k in ks for i in range(chunks[k][2])]
        raw = [pan[d, l].reshape(2 * band, band) for d, l in at]
        for (d, l), (v_hi, v_lo, p_hi, p_lo) in zip(at, factor_panels(raw)):
            vv[d, l, 0] = v_hi
            vv[d, l, 1] = v_lo
            pp[d, l, 0] = p_hi
            pp[d, l, 1] = p_lo

    def apply(d, l, upper, lower):
        s_hi, s_lo = split(jnp.concatenate([upper, lower], axis=0))
        p_hi, p_lo = pp[d, l, 0], pp[d, l, 1]
        v_hi, v_lo = vv[d, l, 0], vv[d, l, 1]
        w_hi, w_lo = split(mm(p_hi, s_hi) + mm(p_hi, s_lo) + mm(p_lo, s_hi))
        change = mm(jnp.concatenate([v_hi, v_lo], axis=1), jnp.concatenate([w_hi, w_hi], axis=0)) + mm(v_hi, w_lo)
        active = flags[d, l] >= 0
        return (jnp.where(active, upper - change[:band], upper), jnp.where(active, lower - change[band:], lower))

    give(0)
    tiles_in.wait()
    for i in range(n_once):
        upward(0, xin.at[once0 + i + shift], u1, i).start()
    give(1)
    near(0)
    give(2)
    near(1)
    give(3)
    far(0)
    flags_copy.wait()
    settle(0)
    factor_chunks(0)
    far(1)
    near(2)

    def early(i, carry):
        upward(0, u1.at[i], u1, i).wait_recv()
        upper, lower = apply(0, twice0 + i, xin[twice0 + i], u1[i])
        s1[i] = lower
        xb[i] = upper
        downward(0, s1.at[i], d1, i).start()

        @pl.when(jnp.logical_not(first))
        def _():
            upward(1, xb.at[i], us, i).start()

        @pl.when(first & (i > 0))
        def _():
            upward(1, xb.at[i], us, i - 1).start()

        return carry

    lax.fori_loop(0, n_twice - held, early, 0)
    near(3)
    far(2)
    settle(1)
    settle(2)
    factor_chunks(1, 2)
    lax.fori_loop(n_twice - held, n_twice, early, 0)
    far(3)

    def middle(i, carry):
        l = once0 + i
        closed = last & (i == n_once - 1)

        @pl.when(first & (i == 0))
        def _():
            xq[...] = xin[once0]

        @pl.when(jnp.logical_not(first & (i == 0)))
        def _():
            j = i - shift
            downward(0, d1.at[j], d1, j).wait_recv()
            xq[...] = d1[j]

        @pl.when(jnp.logical_not(closed))
        def _():
            upward(1, us.at[i], us, i).wait_recv()
            xc[...] = us[i]

        upper, lower = apply(0, l, xq[...], xc[...])
        upper, lower = apply(1, l, upper, lower)
        ss[i] = lower
        xs[i] = upper

        @pl.when(jnp.logical_not(closed))
        def _():
            downward(1, ss.at[i], ds, i).start()

        @pl.when(jnp.logical_not(first & (i == 0)))
        def _():
            upward(2, xs.at[i], u2, i - shift).start()

        return carry

    lax.fori_loop(0, 1, middle, 0)
    settle(3)
    factor_chunks(3)
    lax.fori_loop(1, n_once, middle, 0)

    @pl.when(first)
    def _():
        downward(0, d1.at[n_once - 1], d1, n_once - 1).wait_recv()
        xq[...] = jnp.where(flags[0, twice0] >= 0, xb[0], d1[n_once - 1])
        upward(2, xq, u2, n_once - 1).start()

    def late(i, carry):
        @pl.when(jnp.logical_not(first & (i == 0)))
        def _():
            j = i - shift
            downward(1, ds.at[j], ds, j).wait_recv()
            xc[...] = ds[j]

        @pl.when(first & (i == 0))
        def _():
            xc[...] = xq[...]

        upward(2, u2.at[i], u2, i).wait_recv()
        upper, lower = apply(1, twice0 + i, xc[...], u2[i])
        s2[i] = lower
        xf[i] = upper

        @pl.when(last & (i == n_twice - 1))
        def _():
            remote(s2.at[i], d2, dn_send.at[2, i], dn_recv.at[2, i], below, col).start()

        @pl.when(jnp.logical_not(last & (i == n_twice - 1)))
        def _():
            home(i, s2.at[i]).start()

        @pl.when(jnp.logical_not(first & (i == 0)))
        def _():
            pltpu.make_async_copy(xf.at[i], out.at[twice0 + i, 0], out_sem.at[i]).start()

        return carry

    lax.fori_loop(0, n_twice, late, 0)

    def close(i, carry):
        @pl.when(jnp.logical_not(first & (i == 0)))
        def _():
            j = i - shift
            remote(s2.at[j], out.at[once0 + i, 0], dn_send.at[2, j], dn_recv.at[2, j], below, col).wait_recv()

        return carry

    lax.fori_loop(0, n_once, close, 0)

    @pl.when(first)
    def _():
        own = pltpu.make_async_copy(xs.at[0], out.at[once0, 0], out_sem.at[TILES])
        own.start()
        remote(xq, d2, dn_send.at[2, n_once - 1], dn_recv.at[2, n_once - 1], below, col).wait_recv()
        xb[0] = jnp.where(flags[1, twice0] >= 0, xf[0], d2[...])
        pltpu.make_async_copy(xb.at[0], out.at[twice0, 0], out_sem.at[0]).start()
        own.wait()

    def drain_twice(i, carry):
        downward(0, s1.at[i], d1, i).wait_send()
        home(i, s2.at[i]).wait_send()
        pltpu.make_async_copy(xf.at[i], out.at[twice0 + i, 0], out_sem.at[i]).wait()

        @pl.when(jnp.logical_not(first & (i == n_twice - 1)))
        def _():
            upward(1, xb.at[i], us, i).wait_send()

        return carry

    def drain_once(i, carry):
        upward(0, xs.at[i], u1, i).wait_send()
        upward(2, xs.at[i], u2, i).wait_send()

        @pl.when(jnp.logical_not(last & (i == n_once - 1)))
        def _():
            downward(1, ss.at[i], ds, i).wait_send()

        return carry

    lax.fori_loop(0, n_twice, drain_twice, 0)
    lax.fori_loop(0, n_once, drain_once, 0)
    for k in range(4):
        for j in range(3):
            given(k, j).wait_send()
        for j in range(2):
            onward(k, j).wait_send()
        for j in range(4):
            across(k, j, core).wait_send()


def local(n_row, n_x, eigvec, reflectors, sweep_group):
    tiles, _, band, width = eigvec.shape
    rows = reflectors.shape[3]
    diagonals = reflectors.shape[0]
    cap = max(FEWER, tiles - FEWER)
    one, many = pltpu.VMEM((band, width), f32), pltpu.VMEM((cap, band, width), f32)
    dma = pltpu.SemaphoreType.DMA
    hbm = lambda array: pltpu.with_memory_space_constraint(array, pltpu.HBM)
    flags = sweep_group.reshape(sweep_group.shape[:2])
    return pl.pallas_call(
        functools.partial(kernel, n_row, n_x, FEWER),
        out_shape=jax.ShapeDtypeStruct(eigvec.shape, f32),
        in_specs=[pl.BlockSpec(memory_space=pltpu.HBM)] * 3,
        out_specs=pl.BlockSpec(memory_space=pl.ANY),
        scratch_shapes=[
            pltpu.SMEM(flags.shape, jnp.int32),
            pltpu.VMEM((tiles, band, width), f32),
            many, many, many, one, one,
            many, many, many, many, many, many, many, many, one,
            pltpu.VMEM((diagonals, tiles, 2 * n_x, rows, band), f32),
            pltpu.VMEM((diagonals, tiles, 2, 2 * band, band), bf16),
            pltpu.VMEM((diagonals, tiles, 2, band, 2 * band), bf16),
            dma, dma, dma((4,)), dma((4, 3)), dma((4, 3)), dma((4, 2)), dma((4, 2)), dma((4, 4)), dma((4, 4)),
            dma((3, cap)), dma((3, cap)), dma((3, cap)), dma((3, cap)), dma((tiles + 1,)),
        ],
        compiler_params=pltpu.CompilerParams(
            collective_id=0, has_side_effects=True, vmem_limit_bytes=48 * 1024 * 1024),
    )(hbm(eigvec), hbm(reflectors), hbm(flags))


def solution(mesh):
    return jax.shard_map(
        functools.partial(local, mesh.shape["row"], mesh.shape["col"] // 2),
        mesh=mesh,
        in_specs=(
            P(None, "row", None, "col"),
            P(None, None, "row", "col", None),
            P(None, None, "row"),
        ),
        out_specs=P(None, "row", None, "col"),
        check_vma=False,
    )
```

time: 60.2 us -> 61.6 us (1.023)
  Pallas kernels: 59.1 us -> 60.5 us
    pallas_call x1, Pallas kernels: 59.1 us -> 60.5 us  [local(): pl.pallas_call(functools.partial(kernel, n_row, n_x, FEWER), out_shape=ja...]
where the time goes in v2:
time: 61.6 us; the launch traced here: 61.5 us
  Pallas kernels  60.5 us (98%)
  local copies, waits for them, and re-layouts  0.97 us (2%)
    pallas_call x1, Pallas kernels, local(): pl.pallas_call(functools.partial(kernel, n_row, n_x, FEWER), out_shape=ja...  60.5 us

profile of v2, /device:TPU:1, one launch (start us, length us, event | category | flops | bytes accessed | tf_op | source)
XLA Modules:
  0.0 61.5 jit_solution(9050291439028515897)
XLA Ops:
  0.0 60.5 %shard_map.37 = f32[8,1,128,256]{3,2,1,0:T(8,128)S(1)} custom-call(f32[8,1,128,256]{3,2,1,0:T(8,128)} %refs_0_.1, f32[2,8,1,32,128]{4,3,2,1,0:T(8,128)} %refs_1_.1, s32[2,8]{1,0:T(2,128)} %bitcast.1), custom_call_target="tpu_custom_call" | custom-call | tf_op jit(solution)/shard_map/pallas_call | solution.py:391
  60.5 1.0 %copy.5 = f32[8,1,128,256]{3,2,1,0:T(8,128)} copy(f32[8,1,128,256]{3,2,1,0:T(8,128)S(1)} %shard_map.37) | data formatting | bytes 2097152

commit v3 on v2

--- a/solution.py
+++ b/solution.py
@@ -9,7 +9,7 @@
 
 MESH = pl.DeviceIdType.MESH
 f32, bf16 = jnp.float32, jnp.bfloat16
-TILES, FEWER = 8, 3
+TILES, FEWER = 8, 4
 
 
 def split(a):
@@ -88,16 +88,16 @@
 
     @pl.when(odd)
     def _():
-        body(n_row, n_x, (0, fewer), (fewer, TILES - fewer), 0, *refs)
+        body(n_row, n_x, (0, fewer), (fewer, TILES - fewer), *refs)
 
     @pl.when(jnp.logical_not(odd))
     def _():
-        body(n_row, n_x, (fewer, TILES - fewer), (0, fewer), 1, *refs)
-
-
-def body(n_row, n_x, twice, once, held, eig, refl, flags_in, out,
+        body(n_row, n_x, (fewer, TILES - fewer), (0, fewer), *refs)
+
+
+def body(n_row, n_x, twice, once, eig, refl, flags_in, out,
          flags, xin, xb, xs, xf, xq, xc, u1, us, u2, s1, ss, s2, d1, ds, d2, pan, vv, pp,
-         flag_sem, in_sem, pan_in, pan_send, pan_recv, fwd_send, fwd_recv, rel_send, rel_recv,
+         flag_sem, in_sem, pan_in, pan_send, pan_recv, rel_send, rel_recv,
          up_send, up_recv, dn_send, dn_recv, out_sem):
     row = lax.axis_index("row")
     col = lax.axis_index("col")
@@ -112,14 +112,14 @@
     (twice0, n_twice), (once0, n_once) = twice, once
     partner = x * 2 + (1 - core)
     x_right, x_left, x_far = lax.rem(x + 1, n_x), lax.rem(x + n_x - 1, n_x), lax.rem(x + 2, n_x)
-    right, left = x_right * 2 + core, x_left * 2 + core
-
-    chunks = ((0, *twice), (0, *once), (1, *once), (1, *twice))
-
-    def shares(k, c, half=None):
+    right, left, far = x_right * 2 + core, x_left * 2 + core, x_far * 2 + core
+
+    lead = n_twice // 2
+    chunks = ((0, twice0, lead), (0, twice0 + lead, n_twice - lead), (0, *once), (1, *once), (1, *twice))
+
+    def shares(k, c):
         d, l0, n = chunks[k]
-        lo, hi = {None: (0, n), 0: (0, n // 2), 1: (n // 2, n)}[half]
-        return pan.at[d, pl.ds(l0 + lo, hi - lo), c]
+        return pan.at[d, pl.ds(l0, n), c]
 
     tiles_in = pltpu.make_async_copy(eig.at[:, 0], xin, in_sem)
     tiles_in.start()
@@ -132,9 +132,9 @@
     flags_copy.start()
 
     barrier = pltpu.get_barrier_semaphore()
-    for r_, c_ in ((above, col), (below, col), (row, right), (row, left), (row, partner)):
+    for r_, c_ in ((above, col), (below, col), (row, right), (row, left), (row, far), (row, partner)):
         pl.semaphore_signal(barrier, inc=1, device_id=(r_, c_), device_id_type=MESH)
-    pl.semaphore_wait(barrier, 5)
+    pl.semaphore_wait(barrier, 6)
 
     def remote(src, dst, ssem, rsem, r_, c_):
         return pltpu.make_async_remote_copy(src_ref=src, dst_ref=dst, send_sem=ssem, recv_sem=rsem,
@@ -151,44 +151,29 @@
 
     def given(k, j):
         c = shares(k, col)
-        return remote(c, c, pan_send.at[k, j], pan_recv.at[k, j], row, (right, left, partner)[j])
+        return remote(c, c, pan_send.at[k, j], pan_recv.at[k, j], row, (right, left, far, partner)[j])
 
     def taken(k, j):
-        c = shares(k, (left, right, partner)[j])
+        c = shares(k, (left, right, far, partner)[j])
         return remote(c, c, pan_send.at[k, j], pan_recv.at[k, j], row, partner)
 
-    def onward(k, j):
-        c = shares(k, (left, right)[j], j)
-        return remote(c, c, fwd_send.at[k, j], fwd_recv.at[k, j], row, (right, left)[j])
-
-    def onward_taken(k, j):
-        c = shares(k, x_far * 2 + core, j)
-        return remote(c, c, fwd_send.at[k, j], fwd_recv.at[k, j], row, partner)
-
     def across(k, j, c_):
-        origin = (x_left, x_right, x_far, x_far)[j] * 2 + c_
-        c = shares(k, origin, None if j < 2 else j - 2)
+        c = shares(k, (x_left, x_right, x_far)[j] * 2 + c_)
         return remote(c, c, rel_send.at[k, j], rel_recv.at[k, j], row, partner)
 
     def give(k):
         panels_in[k].wait()
+        for j in (2, 0, 1, 3):
+            given(k, j).start()
+
+    def pass_on(k):
+        for j in (0, 1, 2):
+            taken(k, j).wait_recv()
+            across(k, j, core).start()
+
+    def settle(k):
+        taken(k, 3).wait_recv()
         for j in range(3):
-            given(k, j).start()
-
-    def near(k):
-        for j in range(2):
-            taken(k, j).wait_recv()
-            onward(k, j).start()
-            across(k, j, core).start()
-
-    def far(k):
-        for j in range(2):
-            onward_taken(k, j).wait_recv()
-            across(k, 2 + j, core).start()
-
-    def settle(k):
-        taken(k, 2).wait_recv()
-        for j in range(4):
             across(k, j, 1 - core).wait_recv()
 
     def factor_chunks(*ks):
@@ -213,17 +198,13 @@
     tiles_in.wait()
     for i in range(n_once):
         upward(0, xin.at[once0 + i + shift], u1, i).start()
-    give(1)
-    near(0)
-    give(2)
-    near(1)
-    give(3)
-    far(0)
+    for k in range(1, len(chunks)):
+        give(k)
+    pass_on(0)
     flags_copy.wait()
     settle(0)
     factor_chunks(0)
-    far(1)
-    near(2)
+    pass_on(1)
 
     def early(i, carry):
         upward(0, u1.at[i], u1, i).wait_recv()
@@ -242,14 +223,17 @@
 
         return carry
 
-    lax.fori_loop(0, n_twice - held, early, 0)
-    near(3)
-    far(2)
+    lax.fori_loop(0, lead, early, 0)
+    pass_on(2)
     settle(1)
+    factor_chunks(1)
+    pass_on(3)
+    lax.fori_loop(lead, n_twice - 1, early, 0)
     settle(2)
-    factor_chunks(1, 2)
-    lax.fori_loop(n_twice - held, n_twice, early, 0)
-    far(3)
+    settle(3)
+    factor_chunks(2, 3)
+    lax.fori_loop(n_twice - 1, n_twice, early, 0)
+    pass_on(4)
 
     def middle(i, carry):
         l = once0 + i
@@ -285,10 +269,10 @@
 
         return carry
 
-    lax.fori_loop(0, 1, middle, 0)
-    settle(3)
-    factor_chunks(3)
-    lax.fori_loop(1, n_once, middle, 0)
+    lax.fori_loop(0, 2, middle, 0)
+    settle(4)
+    factor_chunks(4)
+    lax.fori_loop(2, n_once, middle, 0)
 
     @pl.when(first)
     def _():
@@ -370,12 +354,10 @@
 
     lax.fori_loop(0, n_twice, drain_twice, 0)
     lax.fori_loop(0, n_once, drain_once, 0)
-    for k in range(4):
+    for k in range(len(chunks)):
+        for j in range(4):
+            given(k, j).wait_send()
         for j in range(3):
-            given(k, j).wait_send()
-        for j in range(2):
-            onward(k, j).wait_send()
-        for j in range(4):
             across(k, j, core).wait_send()
 
 
@@ -401,7 +383,7 @@
             pltpu.VMEM((diagonals, tiles, 2 * n_x, rows, band), f32),
             pltpu.VMEM((diagonals, tiles, 2, 2 * band, band), bf16),
             pltpu.VMEM((diagonals, tiles, 2, band, 2 * band), bf16),
-            dma, dma, dma((4,)), dma((4, 3)), dma((4, 3)), dma((4, 2)), dma((4, 2)), dma((4, 4)), dma((4, 4)),
+            dma, dma, dma((5,)), dma((5, 4)), dma((5, 4)), dma((5, 3)), dma((5, 3)),
             dma((3, cap)), dma((3, cap)), dma((3, cap)), dma((3, cap)), dma((tiles + 1,)),
         ],
         compiler_params=pltpu.CompilerParams(

time: 61.6 us -> 56.1 us (0.911)
  Pallas kernels: 60.5 us -> 55 us
    pallas_call x1, Pallas kernels: 60.5 us -> 55 us  [local(): pl.pallas_call(functools.partial(kernel, n_row, n_x, FEWER), out_shape=ja...]
where the time goes in v3:
time: 56.1 us; the launch traced here: 56 us
  Pallas kernels  55 us (98%)
  local copies, waits for them, and re-layouts  0.97 us (2%)
    pallas_call x1, Pallas kernels, local(): pl.pallas_call(functools.partial(kernel, n_row, n_x, FEWER), out_shape=ja...  55 us

profile of v3, /device:TPU:1, one launch (start us, length us, event | category | flops | bytes accessed | tf_op | source)
XLA Modules:
  0.0 56.0 jit_solution(12188963657335445285)
XLA Ops:
  0.0 55.0 %shard_map.37 = f32[8,1,128,256]{3,2,1,0:T(8,128)S(1)} custom-call(f32[8,1,128,256]{3,2,1,0:T(8,128)} %refs_0_.1, f32[2,8,1,32,128]{4,3,2,1,0:T(8,128)} %refs_1_.1, s32[2,8]{1,0:T(2,128)} %bitcast.1), custom_call_target="tpu_custom_call" | custom-call | tf_op jit(solution)/shard_map/pallas_call | solution.py:373
  55.0 1.0 %copy.5 = f32[8,1,128,256]{3,2,1,0:T(8,128)} copy(f32[8,1,128,256]{3,2,1,0:T(8,128)S(1)} %shard_map.37) | data formatting | bytes 2097152

commit v4 on v3

--- a/solution.py
+++ b/solution.py
@@ -96,8 +96,8 @@
 
 
 def body(n_row, n_x, twice, once, eig, refl, flags_in, out,
-         flags, xin, xb, xs, xf, xq, xc, u1, us, u2, s1, ss, s2, d1, ds, d2, pan, vv, pp,
-         flag_sem, in_sem, pan_in, pan_send, pan_recv, rel_send, rel_recv,
+         flags, flags_above, xin, xb, xs, xf, xq, xc, u1, us, u2, s1, ss, s2, d1, ds, d2, l1, pan, vv, pp, epan, ev, ep,
+         flag_sem, twin_send, twin_recv, l1_send, l1_recv, in_sem, pan_in, pan_send, pan_recv, rel_send, rel_recv,
          up_send, up_recv, dn_send, dn_recv, out_sem):
     row = lax.axis_index("row")
     col = lax.axis_index("col")
@@ -115,9 +115,12 @@
     right, left, far = x_right * 2 + core, x_left * 2 + core, x_far * 2 + core
 
     lead = n_twice // 2
+    n_both, n_both_above = n_twice - 2, n_once - 2
     chunks = ((0, twice0, lead), (0, twice0 + lead, n_twice - lead), (0, *once), (1, *once), (1, *twice))
 
     def shares(k, c):
+        if k == len(chunks):
+            return epan.at[pl.ds(0, n_both_above), c]
         d, l0, n = chunks[k]
         return pan.at[d, pl.ds(l0, n), c]
 
@@ -161,8 +164,19 @@
         c = shares(k, (x_left, x_right, x_far)[j] * 2 + c_)
         return remote(c, c, rel_send.at[k, j], rel_recv.at[k, j], row, partner)
 
+    def twin_panels(n):
+        return remote(pan.at[0, pl.ds(twice0 + 1, n), col], epan.at[pl.ds(0, n), col], twin_send.at[0], twin_recv.at[0], below, col)
+
+    twin_flags = remote(flags_in, flags_above, twin_send.at[1], twin_recv.at[1], below, col)
+
+    def twin_tile(i):
+        return remote(xin.at[twice0 + 1 + i], l1.at[i], l1_send.at[i], l1_recv.at[i], below, col)
+
     def give(k):
-        panels_in[k].wait()
+        if k == len(chunks):
+            twin_panels(n_both_above).wait_recv()
+        else:
+            panels_in[k].wait()
         for j in (2, 0, 1, 3):
             given(k, j).start()
 
@@ -176,21 +190,33 @@
         for j in range(3):
             across(k, j, 1 - core).wait_recv()
 
-    def factor_chunks(*ks):
+    def factor_chunks(*ks, with_above=False):
         at = [(chunks[k][0], chunks[k][1] + i) for k in ks for i in range(chunks[k][2])]
         raw = [pan[d, l].reshape(2 * band, band) for d, l in at]
-        for (d, l), (v_hi, v_lo, p_hi, p_lo) in zip(at, factor_panels(raw)):
+        if with_above:
+            raw += [epan[e].reshape(2 * band, band) for e in range(n_both_above)]
+        results = factor_panels(raw)
+        for (d, l), (v_hi, v_lo, p_hi, p_lo) in zip(at, results):
             vv[d, l, 0] = v_hi
             vv[d, l, 1] = v_lo
             pp[d, l, 0] = p_hi
             pp[d, l, 1] = p_lo
 
+        if with_above:
+            for e, (v_hi, v_lo, p_hi, p_lo) in enumerate(results[len(at):]):
+                present = flags_above[0:1, once0 + 1 + e:once0 + 2 + e] >= 0
+                ev[e, 0] = v_hi[band:]
+                ev[e, 1] = v_lo[band:]
+                ep[e, 0] = jnp.where(present, p_hi.astype(f32), 0.0).astype(bf16)
+                ep[e, 1] = jnp.where(present, p_lo.astype(f32), 0.0).astype(bf16)
+
+    def change_of(v_hi, v_lo, p_hi, p_lo, upper, lower):
+        s_hi, s_lo = split(jnp.concatenate([upper, lower], axis=0))
+        w_hi, w_lo = split(mm(p_hi, s_hi) + mm(p_hi, s_lo) + mm(p_lo, s_hi))
+        return mm(jnp.concatenate([v_hi, v_lo], axis=1), jnp.concatenate([w_hi, w_hi], axis=0)) + mm(v_hi, w_lo)
+
     def apply(d, l, upper, lower):
-        s_hi, s_lo = split(jnp.concatenate([upper, lower], axis=0))
-        p_hi, p_lo = pp[d, l, 0], pp[d, l, 1]
-        v_hi, v_lo = vv[d, l, 0], vv[d, l, 1]
-        w_hi, w_lo = split(mm(p_hi, s_hi) + mm(p_hi, s_lo) + mm(p_lo, s_hi))
-        change = mm(jnp.concatenate([v_hi, v_lo], axis=1), jnp.concatenate([w_hi, w_hi], axis=0)) + mm(v_hi, w_lo)
+        change = change_of(vv[d, l, 0], vv[d, l, 1], pp[d, l, 0], pp[d, l, 1], upper, lower)
         active = flags[d, l] >= 0
         return (jnp.where(active, upper - change[:band], upper), jnp.where(active, lower - change[band:], lower))
 
@@ -198,7 +224,12 @@
     tiles_in.wait()
     for i in range(n_once):
         upward(0, xin.at[once0 + i + shift], u1, i).start()
-    for k in range(1, len(chunks)):
+    give(1)
+    twin_panels(n_both).start()
+    twin_flags.start()
+    for i in range(n_both):
+        twin_tile(i).start()
+    for k in range(2, len(chunks) + 1):
         give(k)
     pass_on(0)
     flags_copy.wait()
@@ -211,7 +242,10 @@
         upper, lower = apply(0, twice0 + i, xin[twice0 + i], u1[i])
         s1[i] = lower
         xb[i] = upper
-        downward(0, s1.at[i], d1, i).start()
+
+        @pl.when((i == 0) | (i == n_twice - 1))
+        def _():
+            downward(0, s1.at[i], d1, i).start()
 
         @pl.when(jnp.logical_not(first))
         def _():
@@ -234,6 +268,7 @@
     factor_chunks(2, 3)
     lax.fori_loop(n_twice - 1, n_twice, early, 0)
     pass_on(4)
+    pass_on(5)
 
     def middle(i, carry):
         l = once0 + i
@@ -243,11 +278,19 @@
         def _():
             xq[...] = xin[once0]
 
-        @pl.when(jnp.logical_not(first & (i == 0)))
-        def _():
-            j = i - shift
+        j = i - shift
+
+        @pl.when((j == 0) | (j == n_once - 1))
+        def _():
             downward(0, d1.at[j], d1, j).wait_recv()
             xq[...] = d1[j]
+
+        @pl.when((j > 0) & (j < n_once - 1))
+        def _():
+            e = j - 1
+            twin_tile(e).wait_recv()
+            own = xin[once0 + i]
+            xq[...] = own - change_of(ev[e, 0], ev[e, 1], ep[e, 0], ep[e, 1], l1[e], own)
 
         @pl.when(jnp.logical_not(closed))
         def _():
@@ -269,10 +312,12 @@
 
         return carry
 
-    lax.fori_loop(0, 2, middle, 0)
+    lax.fori_loop(0, 1, middle, 0)
     settle(4)
-    factor_chunks(4)
-    lax.fori_loop(2, n_once, middle, 0)
+    settle(5)
+    twin_flags.wait_recv()
+    factor_chunks(4, with_above=True)
+    lax.fori_loop(1, n_once, middle, 0)
 
     @pl.when(first)
     def _():
@@ -332,7 +377,10 @@
         own.wait()
 
     def drain_twice(i, carry):
-        downward(0, s1.at[i], d1, i).wait_send()
+        @pl.when((i == 0) | (i == n_twice - 1))
+        def _():
+            downward(0, s1.at[i], d1, i).wait_send()
+
         home(i, s2.at[i]).wait_send()
         pltpu.make_async_copy(xf.at[i], out.at[twice0 + i, 0], out_sem.at[i]).wait()
 
@@ -354,7 +402,11 @@
 
     lax.fori_loop(0, n_twice, drain_twice, 0)
     lax.fori_loop(0, n_once, drain_once, 0)
-    for k in range(len(chunks)):
+    twin_panels(n_both).wait_send()
+    twin_flags.wait_send()
+    for i in range(n_both):
+        twin_tile(i).wait_send()
+    for k in range(len(chunks) + 1):
         for j in range(4):
             given(k, j).wait_send()
         for j in range(3):
@@ -367,6 +419,7 @@
     diagonals = reflectors.shape[0]
     cap = max(FEWER, tiles - FEWER)
     one, many = pltpu.VMEM((band, width), f32), pltpu.VMEM((cap, band, width), f32)
+    few = pltpu.VMEM((cap - 2, band, width), f32)
     dma = pltpu.SemaphoreType.DMA
     hbm = lambda array: pltpu.with_memory_space_constraint(array, pltpu.HBM)
     flags = sweep_group.reshape(sweep_group.shape[:2])
@@ -377,13 +430,18 @@
         out_specs=pl.BlockSpec(memory_space=pl.ANY),
         scratch_shapes=[
             pltpu.SMEM(flags.shape, jnp.int32),
+            pltpu.VMEM(flags.shape, jnp.int32),
             pltpu.VMEM((tiles, band, width), f32),
             many, many, many, one, one,
-            many, many, many, many, many, many, many, many, one,
+            many, many, many, many, many, many, many, many, one, few,
             pltpu.VMEM((diagonals, tiles, 2 * n_x, rows, band), f32),
             pltpu.VMEM((diagonals, tiles, 2, 2 * band, band), bf16),
             pltpu.VMEM((diagonals, tiles, 2, band, 2 * band), bf16),
-            dma, dma, dma((5,)), dma((5, 4)), dma((5, 4)), dma((5, 3)), dma((5, 3)),
+            pltpu.VMEM((cap - 2, 2 * n_x, rows, band), f32),
+            pltpu.VMEM((cap - 2, 2, band, band), bf16),
+            pltpu.VMEM((cap - 2, 2, band, 2 * band), bf16),
+            dma, dma((2,)), dma((2,)), dma((cap - 2,)), dma((cap - 2,)),
+            dma, dma((5,)), dma((6, 4)), dma((6, 4)), dma((6, 3)), dma((6, 3)),
             dma((3, cap)), dma((3, cap)), dma((3, cap)), dma((3, cap)), dma((tiles + 1,)),
         ],
         compiler_params=pltpu.CompilerParams(

time: 56.1 us -> 57 us (1.016)
  Pallas kernels: 55 us -> 55.9 us
    pallas_call x1, Pallas kernels: 55 us -> 55.9 us  [local(): pl.pallas_call(functools.partial(kernel, n_row, n_x, FEWER), out_shape=ja...]
where the time goes in v4:
time: 57 us; the launch traced here: 56.9 us
  Pallas kernels  55.9 us (98%)
  local copies, waits for them, and re-layouts  0.97 us (2%)
    pallas_call x1, Pallas kernels, local(): pl.pallas_call(functools.partial(kernel, n_row, n_x, FEWER), out_shape=ja...  55.9 us

profile of v4, /device:TPU:1, one launch (start us, length us, event | category | flops | bytes accessed | tf_op | source)
XLA Modules:
  0.0 56.9 jit_solution(8224980217320301230)
XLA Ops:
  0.0 55.9 %shard_map.37 = f32[8,1,128,256]{3,2,1,0:T(8,128)S(1)} custom-call(f32[8,1,128,256]{3,2,1,0:T(8,128)} %refs_0_.1, f32[2,8,1,32,128]{4,3,2,1,0:T(8,128)} %refs_1_.1, s32[2,8]{1,0:T(2,128)} %bitcast.1), custom_call_target="tpu_custom_call" | custom-call | tf_op jit(solution)/shard_map/pallas_call | solution.py:426
  55.9 1.0 %copy.5 = f32[8,1,128,256]{3,2,1,0:T(8,128)} copy(f32[8,1,128,256]{3,2,1,0:T(8,128)S(1)} %shard_map.37) | data formatting | bytes 2097152

commit v5 on v4

--- a/solution.py
+++ b/solution.py
@@ -9,7 +9,7 @@
 
 MESH = pl.DeviceIdType.MESH
 f32, bf16 = jnp.float32, jnp.bfloat16
-TILES, FEWER = 8, 4
+TILES, FEWER, BOTH = 8, 4, 1
 
 
 def split(a):
@@ -96,7 +96,7 @@
 
 
 def body(n_row, n_x, twice, once, eig, refl, flags_in, out,
-         flags, flags_above, xin, xb, xs, xf, xq, xc, u1, us, u2, s1, ss, s2, d1, ds, d2, l1, pan, vv, pp, epan, ev, ep,
+         flags, flags_above, xin, xb, xs, xf, xq, xc, xz, u1, us, u2, s1, ss, s2, d1, ds, d2, l1, pan, vv, pp, epan, ev, ep,
          flag_sem, twin_send, twin_recv, l1_send, l1_recv, in_sem, pan_in, pan_send, pan_recv, rel_send, rel_recv,
          up_send, up_recv, dn_send, dn_recv, out_sem):
     row = lax.axis_index("row")
@@ -112,22 +112,36 @@
     (twice0, n_twice), (once0, n_once) = twice, once
     partner = x * 2 + (1 - core)
     x_right, x_left, x_far = lax.rem(x + 1, n_x), lax.rem(x + n_x - 1, n_x), lax.rem(x + 2, n_x)
-    right, left, far = x_right * 2 + core, x_left * 2 + core, x_far * 2 + core
-
-    lead = n_twice // 2
-    n_both, n_both_above = n_twice - 2, n_once - 2
-    chunks = ((0, twice0, lead), (0, twice0 + lead, n_twice - lead), (0, *once), (1, *once), (1, *twice))
+    right, left, far = x_right * 2 + 1, x_left * 2 + 1, x_far * 2 + 1
+
+    both, lead = epan.shape[0], n_twice // 2
+    half = n_once // 2
+    chunks = ((0, twice0 + lead, n_twice - lead),
+              (0, once0 + half, n_once - half), (1, once0 + half, n_once - half),
+              (0, twice0, lead),
+              (0, once0, half), (1, once0, half),
+              None,
+              (1, *twice))
+    order = range(n_twice - 1, -1, -1)
+
+    def ordered(p):
+        return n_twice - 1 - p
+
 
     def shares(k, c):
-        if k == len(chunks):
-            return epan.at[pl.ds(0, n_both_above), c]
+        if chunks[k] is None:
+            return epan.at[:, c]
         d, l0, n = chunks[k]
         return pan.at[d, pl.ds(l0, n), c]
 
     tiles_in = pltpu.make_async_copy(eig.at[:, 0], xin, in_sem)
     tiles_in.start()
     panels_in = []
-    for k, (d, l0, n) in enumerate(chunks):
+    for k, chunk in enumerate(chunks):
+        if chunk is None:
+            panels_in.append(None)
+            continue
+        d, l0, n = chunk
         copy = pltpu.make_async_copy(refl.at[d, pl.ds(l0, n), 0], shares(k, col), pan_in.at[k])
         copy.start()
         panels_in.append(copy)
@@ -135,8 +149,15 @@
     flags_copy.start()
 
     barrier = pltpu.get_barrier_semaphore()
-    for r_, c_ in ((above, col), (below, col), (row, right), (row, left), (row, far), (row, partner)):
+    for r_, c_ in ((above, col), (below, col), (row, partner)):
         pl.semaphore_signal(barrier, inc=1, device_id=(r_, c_), device_id_type=MESH)
+
+    @pl.when(core == 1)
+    def _():
+        for x_ in (x_right, x_left, x_far):
+            for c_ in range(2):
+                pl.semaphore_signal(barrier, inc=1, device_id=(row, x_ * 2 + c_), device_id_type=MESH)
+
     pl.semaphore_wait(barrier, 6)
 
     def remote(src, dst, ssem, rsem, r_, c_):
@@ -154,47 +175,62 @@
 
     def given(k, j):
         c = shares(k, col)
-        return remote(c, c, pan_send.at[k, j], pan_recv.at[k, j], row, (right, left, far, partner)[j])
-
-    def taken(k, j):
-        c = shares(k, (left, right, far, partner)[j])
-        return remote(c, c, pan_send.at[k, j], pan_recv.at[k, j], row, partner)
+        return remote(c, c, pan_send.at[k, j], pan_recv.at[k, 2 * j + core], row, (right, left, far)[j])
+
+    def given_partner(k):
+        c = shares(k, col)
+        return remote(c, c, pan_send.at[k, 3], pan_recv.at[k, 6], row, partner)
+
+    def taken(k, j, c_):
+        c = shares(k, (x_left, x_right, x_far)[j] * 2 + c_)
+        return remote(c, c, pan_send.at[k, j], pan_recv.at[k, 2 * j + c_], row, partner)
+
+    def taken_partner(k):
+        c = shares(k, partner)
+        return remote(c, c, pan_send.at[k, 3], pan_recv.at[k, 6], row, partner)
 
     def across(k, j, c_):
         c = shares(k, (x_left, x_right, x_far)[j] * 2 + c_)
-        return remote(c, c, rel_send.at[k, j], rel_recv.at[k, j], row, partner)
-
-    def twin_panels(n):
-        return remote(pan.at[0, pl.ds(twice0 + 1, n), col], epan.at[pl.ds(0, n), col], twin_send.at[0], twin_recv.at[0], below, col)
-
+        return remote(c, c, rel_send.at[k, 2 * j + c_], rel_recv.at[k, 2 * j + c_], row, partner)
+
+    arrivals = [(j, c_) for j in range(3) for c_ in (1, 0)]
+
+    twin_panels = remote(pan.at[0, pl.ds(twice0, both), col], epan.at[:, col], twin_send.at[0], twin_recv.at[0], below, col)
     twin_flags = remote(flags_in, flags_above, twin_send.at[1], twin_recv.at[1], below, col)
 
-    def twin_tile(i):
-        return remote(xin.at[twice0 + 1 + i], l1.at[i], l1_send.at[i], l1_recv.at[i], below, col)
+    def twin_tile(e):
+        return remote(xin.at[twice0 + e], l1.at[e], l1_send.at[e], l1_recv.at[e], below, col)
 
     def give(k):
-        if k == len(chunks):
-            twin_panels(n_both_above).wait_recv()
+        if chunks[k] is None:
+            twin_panels.wait_recv()
         else:
             panels_in[k].wait()
-        for j in (2, 0, 1, 3):
+        given_partner(k).start()
+        for j in (2, 0, 1):
             given(k, j).start()
 
     def pass_on(k):
-        for j in (0, 1, 2):
-            taken(k, j).wait_recv()
-            across(k, j, core).start()
+        @pl.when(core == 1)
+        def _():
+            for j, c_ in arrivals:
+                taken(k, j, c_).wait_recv()
+                across(k, j, c_).start()
 
     def settle(k):
-        taken(k, 3).wait_recv()
-        for j in range(3):
-            across(k, j, 1 - core).wait_recv()
-
-    def factor_chunks(*ks, with_above=False):
-        at = [(chunks[k][0], chunks[k][1] + i) for k in ks for i in range(chunks[k][2])]
+        taken_partner(k).wait_recv()
+
+        @pl.when(core == 0)
+        def _():
+            for j, c_ in arrivals:
+                across(k, j, c_).wait_recv()
+
+    def factor_chunks(*ks):
+        with_above = any(chunks[k] is None for k in ks)
+        at = [(chunks[k][0], chunks[k][1] + i) for k in ks if chunks[k] for i in range(chunks[k][2])]
         raw = [pan[d, l].reshape(2 * band, band) for d, l in at]
         if with_above:
-            raw += [epan[e].reshape(2 * band, band) for e in range(n_both_above)]
+            raw += [epan[e].reshape(2 * band, band) for e in range(both)]
         results = factor_panels(raw)
         for (d, l), (v_hi, v_lo, p_hi, p_lo) in zip(at, results):
             vv[d, l, 0] = v_hi
@@ -204,7 +240,7 @@
 
         if with_above:
             for e, (v_hi, v_lo, p_hi, p_lo) in enumerate(results[len(at):]):
-                present = flags_above[0:1, once0 + 1 + e:once0 + 2 + e] >= 0
+                present = flags_above[0:1, once0 + e:once0 + e + 1] >= 0
                 ev[e, 0] = v_hi[band:]
                 ev[e, 1] = v_lo[band:]
                 ep[e, 0] = jnp.where(present, p_hi.astype(f32), 0.0).astype(bf16)
@@ -222,29 +258,34 @@
 
     give(0)
     tiles_in.wait()
-    for i in range(n_once):
+    for i in order:
         upward(0, xin.at[once0 + i + shift], u1, i).start()
-    give(1)
-    twin_panels(n_both).start()
+    for k in (1, 2, 3):
+        give(k)
+    twin_panels.start()
     twin_flags.start()
-    for i in range(n_both):
-        twin_tile(i).start()
-    for k in range(2, len(chunks) + 1):
+    for e in range(both):
+        twin_tile(e).start()
+    for k in (4, 5):
         give(k)
     pass_on(0)
     flags_copy.wait()
     settle(0)
     factor_chunks(0)
+    give(6)
+    give(7)
     pass_on(1)
-
-    def early(i, carry):
+    pass_on(2)
+
+    def early(p, carry):
+        i = ordered(p)
         upward(0, u1.at[i], u1, i).wait_recv()
         upper, lower = apply(0, twice0 + i, xin[twice0 + i], u1[i])
-        s1[i] = lower
         xb[i] = upper
 
-        @pl.when((i == 0) | (i == n_twice - 1))
-        def _():
+        @pl.when(i >= both)
+        def _():
+            s1[i] = lower
             downward(0, s1.at[i], d1, i).start()
 
         @pl.when(jnp.logical_not(first))
@@ -257,20 +298,25 @@
 
         return carry
 
-    lax.fori_loop(0, lead, early, 0)
-    pass_on(2)
+    lax.fori_loop(0, n_twice - lead, early, 0)
+    pass_on(3)
     settle(1)
-    factor_chunks(1)
-    pass_on(3)
-    lax.fori_loop(lead, n_twice - 1, early, 0)
     settle(2)
     settle(3)
-    factor_chunks(2, 3)
-    lax.fori_loop(n_twice - 1, n_twice, early, 0)
+    factor_chunks(1, 2, 3)
+    lax.fori_loop(n_twice - lead, n_twice, early, 0)
     pass_on(4)
     pass_on(5)
-
-    def middle(i, carry):
+    pass_on(6)
+
+    @pl.when(first)
+    def _():
+        downward(0, d1.at[n_once - 1], d1, n_once - 1).wait_recv()
+        xz[...] = jnp.where(flags[0, twice0] >= 0, xb[0], d1[n_once - 1])
+        upward(2, xz, u2, n_once - 1).start()
+
+    def middle(p, carry):
+        i = ordered(p)
         l = once0 + i
         closed = last & (i == n_once - 1)
 
@@ -280,17 +326,20 @@
 
         j = i - shift
 
-        @pl.when((j == 0) | (j == n_once - 1))
+        @pl.when(j >= both)
         def _():
             downward(0, d1.at[j], d1, j).wait_recv()
             xq[...] = d1[j]
 
-        @pl.when((j > 0) & (j < n_once - 1))
-        def _():
-            e = j - 1
-            twin_tile(e).wait_recv()
+        @pl.when((j >= 0) & (j < both))
+        def _():
+            twin_tile(j).wait_recv()
             own = xin[once0 + i]
-            xq[...] = own - change_of(ev[e, 0], ev[e, 1], ep[e, 0], ep[e, 1], l1[e], own)
+            xq[...] = own - change_of(ev[j, 0], ev[j, 1], ep[j, 0], ep[j, 1], l1[j], own)
+
+        @pl.when(closed)
+        def _():
+            xc[...] = xin[once0]
 
         @pl.when(jnp.logical_not(closed))
         def _():
@@ -312,20 +361,21 @@
 
         return carry
 
-    lax.fori_loop(0, 1, middle, 0)
+    lax.fori_loop(0, n_once - half, middle, 0)
+
     settle(4)
     settle(5)
+    settle(6)
     twin_flags.wait_recv()
-    factor_chunks(4, with_above=True)
-    lax.fori_loop(1, n_once, middle, 0)
-
-    @pl.when(first)
-    def _():
-        downward(0, d1.at[n_once - 1], d1, n_once - 1).wait_recv()
-        xq[...] = jnp.where(flags[0, twice0] >= 0, xb[0], d1[n_once - 1])
-        upward(2, xq, u2, n_once - 1).start()
-
-    def late(i, carry):
+    factor_chunks(4, 5, 6)
+    pass_on(7)
+    lax.fori_loop(n_once - half, n_once, middle, 0)
+    settle(7)
+    factor_chunks(7)
+
+    def late(p, carry):
+        i = ordered(p)
+
         @pl.when(jnp.logical_not(first & (i == 0)))
         def _():
             j = i - shift
@@ -334,7 +384,7 @@
 
         @pl.when(first & (i == 0))
         def _():
-            xc[...] = xq[...]
+            xc[...] = xz[...]
 
         upward(2, u2.at[i], u2, i).wait_recv()
         upper, lower = apply(1, twice0 + i, xc[...], u2[i])
@@ -357,6 +407,45 @@
 
     lax.fori_loop(0, n_twice, late, 0)
 
+    def drain_twice(i, carry):
+        @pl.when(i >= both)
+        def _():
+            downward(0, s1.at[i], d1, i).wait_send()
+
+        @pl.when(i < both)
+        def _():
+            twin_tile(i).wait_send()
+
+        @pl.when(jnp.logical_not(first & (i == n_twice - 1)))
+        def _():
+            upward(1, xb.at[i], us, i).wait_send()
+
+        return carry
+
+    def drain_once(i, carry):
+        upward(0, xs.at[i], u1, i).wait_send()
+        upward(2, xs.at[i], u2, i).wait_send()
+
+        @pl.when(jnp.logical_not(last & (i == n_once - 1)))
+        def _():
+            downward(1, ss.at[i], ds, i).wait_send()
+
+        return carry
+
+    lax.fori_loop(0, n_twice, drain_twice, 0)
+    lax.fori_loop(0, n_once, drain_once, 0)
+    twin_panels.wait_send()
+    twin_flags.wait_send()
+    for k in range(len(chunks)):
+        for j in range(3):
+            given(k, j).wait_send()
+        given_partner(k).wait_send()
+
+        @pl.when(core == 1)
+        def _():
+            for j, c_ in arrivals:
+                across(k, j, c_).wait_send()
+
     def close(i, carry):
         @pl.when(jnp.logical_not(first & (i == 0)))
         def _():
@@ -371,46 +460,17 @@
     def _():
         own = pltpu.make_async_copy(xs.at[0], out.at[once0, 0], out_sem.at[TILES])
         own.start()
-        remote(xq, d2, dn_send.at[2, n_once - 1], dn_recv.at[2, n_once - 1], below, col).wait_recv()
+        remote(xz, d2, dn_send.at[2, n_once - 1], dn_recv.at[2, n_once - 1], below, col).wait_recv()
         xb[0] = jnp.where(flags[1, twice0] >= 0, xf[0], d2[...])
         pltpu.make_async_copy(xb.at[0], out.at[twice0, 0], out_sem.at[0]).start()
         own.wait()
 
-    def drain_twice(i, carry):
-        @pl.when((i == 0) | (i == n_twice - 1))
-        def _():
-            downward(0, s1.at[i], d1, i).wait_send()
-
+    def finish(i, carry):
         home(i, s2.at[i]).wait_send()
         pltpu.make_async_copy(xf.at[i], out.at[twice0 + i, 0], out_sem.at[i]).wait()
-
-        @pl.when(jnp.logical_not(first & (i == n_twice - 1)))
-        def _():
-            upward(1, xb.at[i], us, i).wait_send()
-
-        return carry
-
-    def drain_once(i, carry):
-        upward(0, xs.at[i], u1, i).wait_send()
-        upward(2, xs.at[i], u2, i).wait_send()
-
-        @pl.when(jnp.logical_not(last & (i == n_once - 1)))
-        def _():
-            downward(1, ss.at[i], ds, i).wait_send()
-
-        return carry
-
-    lax.fori_loop(0, n_twice, drain_twice, 0)
-    lax.fori_loop(0, n_once, drain_once, 0)
-    twin_panels(n_both).wait_send()
-    twin_flags.wait_send()
-    for i in range(n_both):
-        twin_tile(i).wait_send()
-    for k in range(len(chunks) + 1):
-        for j in range(4):
-            given(k, j).wait_send()
-        for j in range(3):
-            across(k, j, core).wait_send()
+        return carry
+
+    lax.fori_loop(0, n_twice, finish, 0)
 
 
 def local(n_row, n_x, eigvec, reflectors, sweep_group):
@@ -419,7 +479,7 @@
     diagonals = reflectors.shape[0]
     cap = max(FEWER, tiles - FEWER)
     one, many = pltpu.VMEM((band, width), f32), pltpu.VMEM((cap, band, width), f32)
-    few = pltpu.VMEM((cap - 2, band, width), f32)
+    pair = BOTH
     dma = pltpu.SemaphoreType.DMA
     hbm = lambda array: pltpu.with_memory_space_constraint(array, pltpu.HBM)
     flags = sweep_group.reshape(sweep_group.shape[:2])
@@ -432,16 +492,16 @@
             pltpu.SMEM(flags.shape, jnp.int32),
             pltpu.VMEM(flags.shape, jnp.int32),
             pltpu.VMEM((tiles, band, width), f32),
-            many, many, many, one, one,
-            many, many, many, many, many, many, many, many, one, few,
+            many, many, many, one, one, one,
+            many, many, many, many, many, many, many, many, one, pltpu.VMEM((pair, band, width), f32),
             pltpu.VMEM((diagonals, tiles, 2 * n_x, rows, band), f32),
             pltpu.VMEM((diagonals, tiles, 2, 2 * band, band), bf16),
             pltpu.VMEM((diagonals, tiles, 2, band, 2 * band), bf16),
-            pltpu.VMEM((cap - 2, 2 * n_x, rows, band), f32),
-            pltpu.VMEM((cap - 2, 2, band, band), bf16),
-            pltpu.VMEM((cap - 2, 2, band, 2 * band), bf16),
-            dma, dma((2,)), dma((2,)), dma((cap - 2,)), dma((cap - 2,)),
-            dma, dma((5,)), dma((6, 4)), dma((6, 4)), dma((6, 3)), dma((6, 3)),
+            pltpu.VMEM((pair, 2 * n_x, rows, band), f32),
+            pltpu.VMEM((pair, 2, band, band), bf16),
+            pltpu.VMEM((pair, 2, band, 2 * band), bf16),
+            dma, dma((2,)), dma((2,)), dma((pair,)), dma((pair,)),
+            dma, dma((8,)), dma((8, 4)), dma((8, 7)), dma((8, 6)), dma((8, 6)),
             dma((3, cap)), dma((3, cap)), dma((3, cap)), dma((3, cap)), dma((tiles + 1,)),
         ],
         compiler_params=pltpu.CompilerParams(

time: 57 us -> 54.1 us (0.949); the launches traced: 56.9 us -> 53.2 us
  Pallas kernels: 55.9 us -> 52.2 us
    pallas_call x1, Pallas kernels: 55.9 us -> 52.2 us  [local(): pl.pallas_call(functools.partial(kernel, n_row, n_x, FEWER), out_shape=ja...]
where the time goes in v5:
time: 54.1 us; the launch traced here: 53.2 us
  Pallas kernels  52.2 us (96%)
  local copies, waits for them, and re-layouts  0.97 us (2%)
    pallas_call x1, Pallas kernels, local(): pl.pallas_call(functools.partial(kernel, n_row, n_x, FEWER), out_shape=ja...  52.2 us

profile of v5, /device:TPU:1, one launch (start us, length us, event | category | flops | bytes accessed | tf_op | source)
XLA Modules:
  0.0 53.2 jit_solution(10320946972627062349)
XLA Ops:
  0.0 52.2 %shard_map.37 = f32[8,1,128,256]{3,2,1,0:T(8,128)S(1)} custom-call(f32[8,1,128,256]{3,2,1,0:T(8,128)} %refs_0_.1, f32[2,8,1,32,128]{4,3,2,1,0:T(8,128)} %refs_1_.1, s32[2,8]{1,0:T(2,128)} %bitcast.1), custom_call_target="tpu_custom_call" | custom-call | tf_op jit(solution)/shard_map/pallas_call | solution.py:486
  52.2 1.0 %copy.5 = f32[8,1,128,256]{3,2,1,0:T(8,128)} copy(f32[8,1,128,256]{3,2,1,0:T(8,128)S(1)} %shard_map.37) | data formatting | bytes 2097152

commit v6 on v5

--- a/solution.py
+++ b/solution.py
@@ -97,7 +97,7 @@
 
 def body(n_row, n_x, twice, once, eig, refl, flags_in, out,
          flags, flags_above, xin, xb, xs, xf, xq, xc, xz, u1, us, u2, s1, ss, s2, d1, ds, d2, l1, pan, vv, pp, epan, ev, ep,
-         flag_sem, twin_send, twin_recv, l1_send, l1_recv, in_sem, pan_in, pan_send, pan_recv, rel_send, rel_recv,
+         flag_sem, twin_send, twin_recv, l1_send, l1_recv, in_sem, pan_in, pan_send, pan_recv, rel_send,
          up_send, up_recv, dn_send, dn_recv, out_sem):
     row = lax.axis_index("row")
     col = lax.axis_index("col")
@@ -136,15 +136,8 @@
 
     tiles_in = pltpu.make_async_copy(eig.at[:, 0], xin, in_sem)
     tiles_in.start()
-    panels_in = []
-    for k, chunk in enumerate(chunks):
-        if chunk is None:
-            panels_in.append(None)
-            continue
-        d, l0, n = chunk
-        copy = pltpu.make_async_copy(refl.at[d, pl.ds(l0, n), 0], shares(k, col), pan_in.at[k])
-        copy.start()
-        panels_in.append(copy)
+    panels_in = pltpu.make_async_copy(refl.at[:, :, 0], pan.at[:, :, col], pan_in)
+    panels_in.start()
     flags_copy = pltpu.make_async_copy(flags_in, flags, flag_sem)
     flags_copy.start()
 
@@ -165,33 +158,29 @@
                                             device_id=(r_, c_), device_id_type=MESH)
 
     def upward(kind, src, dst, i):
-        return remote(src, dst.at[i], up_send.at[kind, i], up_recv.at[kind, i], above, col)
+        return remote(src, dst.at[i], up_send.at[kind], up_recv.at[kind, i], above, col)
 
     def downward(kind, src, dst, i):
-        return remote(src, dst.at[i], dn_send.at[kind, i], dn_recv.at[kind, i], below, col)
+        return remote(src, dst.at[i], dn_send.at[kind], dn_recv.at[kind, i], below, col)
 
     def home(i, src):
-        return remote(src, out.at[twice0 + next_shift + i, 0], dn_send.at[2, i], dn_recv.at[2, i], below, col)
+        return remote(src, out.at[twice0 + next_shift + i, 0], dn_send.at[2], dn_recv.at[2, i], below, col)
 
     def given(k, j):
         c = shares(k, col)
-        return remote(c, c, pan_send.at[k, j], pan_recv.at[k, 2 * j + core], row, (right, left, far)[j])
-
-    def given_partner(k):
-        c = shares(k, col)
-        return remote(c, c, pan_send.at[k, 3], pan_recv.at[k, 6], row, partner)
-
-    def taken(k, j, c_):
-        c = shares(k, (x_left, x_right, x_far)[j] * 2 + c_)
-        return remote(c, c, pan_send.at[k, j], pan_recv.at[k, 2 * j + c_], row, partner)
-
-    def taken_partner(k):
-        c = shares(k, partner)
-        return remote(c, c, pan_send.at[k, 3], pan_recv.at[k, 6], row, partner)
+        return remote(c, c, pan_send.at[k], pan_recv.at[k], row, (right, left, far, partner)[j])
 
     def across(k, j, c_):
         c = shares(k, (x_left, x_right, x_far)[j] * 2 + c_)
-        return remote(c, c, rel_send.at[k, 2 * j + c_], rel_recv.at[k, 2 * j + c_], row, partner)
+        return remote(c, c, rel_send.at[k], pan_recv.at[k], row, partner)
+
+    def amount(k, n, send_sem):
+        if chunks[k] is None:
+            c = epan.at[:, pl.ds(0, n)]
+        else:
+            d, l0, m = chunks[k]
+            c = pan.at[d, pl.ds(l0, m), pl.ds(0, n)]
+        return remote(c, c, send_sem.at[k], pan_recv.at[k], row, partner)
 
     arrivals = [(j, c_) for j in range(3) for c_ in (1, 0)]
 
@@ -204,26 +193,20 @@
     def give(k):
         if chunks[k] is None:
             twin_panels.wait_recv()
-        else:
-            panels_in[k].wait()
-        given_partner(k).start()
-        for j in (2, 0, 1):
+        for j in (3, 2, 0, 1):
             given(k, j).start()
 
     def pass_on(k):
         @pl.when(core == 1)
         def _():
+            amount(k, 2 * n_x - 1, pan_send).wait_recv()
             for j, c_ in arrivals:
-                taken(k, j, c_).wait_recv()
                 across(k, j, c_).start()
 
     def settle(k):
-        taken_partner(k).wait_recv()
-
         @pl.when(core == 0)
         def _():
-            for j, c_ in arrivals:
-                across(k, j, c_).wait_recv()
+            amount(k, 2 * n_x - 1, pan_send).wait_recv()
 
     def factor_chunks(*ks):
         with_above = any(chunks[k] is None for k in ks)
@@ -256,6 +239,7 @@
         active = flags[d, l] >= 0
         return (jnp.where(active, upper - change[:band], upper), jnp.where(active, lower - change[band:], lower))
 
+    panels_in.wait()
     give(0)
     tiles_in.wait()
     for i in order:
@@ -393,7 +377,7 @@
 
         @pl.when(last & (i == n_twice - 1))
         def _():
-            remote(s2.at[i], d2, dn_send.at[2, i], dn_recv.at[2, i], below, col).start()
+            remote(s2.at[i], d2, dn_send.at[2], dn_recv.at[2, i], below, col).start()
 
         @pl.when(jnp.logical_not(last & (i == n_twice - 1)))
         def _():
@@ -401,56 +385,54 @@
 
         @pl.when(jnp.logical_not(first & (i == 0)))
         def _():
-            pltpu.make_async_copy(xf.at[i], out.at[twice0 + i, 0], out_sem.at[i]).start()
+            pltpu.make_async_copy(xf.at[i], out.at[twice0 + i, 0], out_sem.at[0]).start()
 
         return carry
 
     lax.fori_loop(0, n_twice, late, 0)
 
-    def drain_twice(i, carry):
-        @pl.when(i >= both)
-        def _():
-            downward(0, s1.at[i], d1, i).wait_send()
-
-        @pl.when(i < both)
-        def _():
-            twin_tile(i).wait_send()
-
-        @pl.when(jnp.logical_not(first & (i == n_twice - 1)))
-        def _():
-            upward(1, xb.at[i], us, i).wait_send()
-
-        return carry
-
-    def drain_once(i, carry):
-        upward(0, xs.at[i], u1, i).wait_send()
-        upward(2, xs.at[i], u2, i).wait_send()
-
-        @pl.when(jnp.logical_not(last & (i == n_once - 1)))
-        def _():
-            downward(1, ss.at[i], ds, i).wait_send()
-
-        return carry
-
-    lax.fori_loop(0, n_twice, drain_twice, 0)
-    lax.fori_loop(0, n_once, drain_once, 0)
+    def left_up(kind, n):
+        remote(xs.at[pl.ds(0, n)], u1.at[pl.ds(0, n)], up_send.at[kind], up_recv.at[kind, 0], above, col).wait_send()
+
+    def left_down(kind, n):
+        remote(xs.at[pl.ds(0, n)], d1.at[pl.ds(0, n)], dn_send.at[kind], dn_recv.at[kind, 0], below, col).wait_send()
+
+    left_up(0, n_once)
+    left_up(2, n_once)
+    left_down(0, n_twice - both)
+
+    @pl.when(first)
+    def _():
+        left_up(1, n_twice - 1)
+
+    @pl.when(jnp.logical_not(first))
+    def _():
+        left_up(1, n_twice)
+
+    @pl.when(last)
+    def _():
+        left_down(1, n_once - 1)
+
+    @pl.when(jnp.logical_not(last))
+    def _():
+        left_down(1, n_once)
+
     twin_panels.wait_send()
     twin_flags.wait_send()
+    for e in range(both):
+        twin_tile(e).wait_send()
     for k in range(len(chunks)):
-        for j in range(3):
-            given(k, j).wait_send()
-        given_partner(k).wait_send()
+        amount(k, n_x, pan_send).wait_send()
 
         @pl.when(core == 1)
         def _():
-            for j, c_ in arrivals:
-                across(k, j, c_).wait_send()
+            amount(k, 2 * n_x - 2, rel_send).wait_send()
 
     def close(i, carry):
         @pl.when(jnp.logical_not(first & (i == 0)))
         def _():
             j = i - shift
-            remote(s2.at[j], out.at[once0 + i, 0], dn_send.at[2, j], dn_recv.at[2, j], below, col).wait_recv()
+            remote(s2.at[j], out.at[once0 + i, 0], dn_send.at[2], dn_recv.at[2, j], below, col).wait_recv()
 
         return carry
 
@@ -458,19 +440,15 @@
 
     @pl.when(first)
     def _():
-        own = pltpu.make_async_copy(xs.at[0], out.at[once0, 0], out_sem.at[TILES])
+        own = pltpu.make_async_copy(xs.at[0], out.at[once0, 0], out_sem.at[1])
         own.start()
-        remote(xz, d2, dn_send.at[2, n_once - 1], dn_recv.at[2, n_once - 1], below, col).wait_recv()
+        remote(xz, d2, dn_send.at[2], dn_recv.at[2, n_once - 1], below, col).wait_recv()
         xb[0] = jnp.where(flags[1, twice0] >= 0, xf[0], d2[...])
         pltpu.make_async_copy(xb.at[0], out.at[twice0, 0], out_sem.at[0]).start()
         own.wait()
 
-    def finish(i, carry):
-        home(i, s2.at[i]).wait_send()
-        pltpu.make_async_copy(xf.at[i], out.at[twice0 + i, 0], out_sem.at[i]).wait()
-        return carry
-
-    lax.fori_loop(0, n_twice, finish, 0)
+    left_down(2, n_twice)
+    pltpu.make_async_copy(xf, out.at[pl.ds(twice0, n_twice), 0], out_sem.at[0]).wait()
 
 
 def local(n_row, n_x, eigvec, reflectors, sweep_group):
@@ -501,8 +479,8 @@
             pltpu.VMEM((pair, 2, band, band), bf16),
             pltpu.VMEM((pair, 2, band, 2 * band), bf16),
             dma, dma((2,)), dma((2,)), dma((pair,)), dma((pair,)),
-            dma, dma((8,)), dma((8, 4)), dma((8, 7)), dma((8, 6)), dma((8, 6)),
-            dma((3, cap)), dma((3, cap)), dma((3, cap)), dma((3, cap)), dma((tiles + 1,)),
+            dma, dma, dma((8,)), dma((8,)), dma((8,)),
+            dma((3,)), dma((3, cap)), dma((3,)), dma((3, cap)), dma((2,)),
         ],
         compiler_params=pltpu.CompilerParams(
             collective_id=0, has_side_effects=True, vmem_limit_bytes=48 * 1024 * 1024),

time: 54.1 us -> 52.4 us (0.969)
  Pallas kernels: 52.2 us -> 50.5 us
    pallas_call x1, Pallas kernels: 52.2 us -> 50.5 us  [local(): pl.pallas_call(functools.partial(kernel, n_row, n_x, FEWER), out_shape=ja...]
where the time goes in v6:
time: 52.4 us; the launch traced here: 51.5 us
  Pallas kernels  50.5 us (96%)
  local copies, waits for them, and re-layouts  0.97 us (2%)
    pallas_call x1, Pallas kernels, local(): pl.pallas_call(functools.partial(kernel, n_row, n_x, FEWER), out_shape=ja...  50.5 us

profile of v6, /device:TPU:1, one launch (start us, length us, event | category | flops | bytes accessed | tf_op | source)
XLA Modules:
  0.0 51.5 jit_solution(14141467685937631608)
XLA Ops:
  0.0 50.5 %shard_map.37 = f32[8,1,128,256]{3,2,1,0:T(8,128)S(1)} custom-call(f32[8,1,128,256]{3,2,1,0:T(8,128)} %refs_0_.1, f32[2,8,1,32,128]{4,3,2,1,0:T(8,128)} %refs_1_.1, s32[2,8]{1,0:T(2,128)} %bitcast.1), custom_call_target="tpu_custom_call" | custom-call | tf_op jit(solution)/shard_map/pallas_call | solution.py:464
  50.5 1.0 %copy.5 = f32[8,1,128,256]{3,2,1,0:T(8,128)} copy(f32[8,1,128,256]{3,2,1,0:T(8,128)S(1)} %shard_map.37) | data formatting | bytes 2097152

commit v7 on v6

--- a/solution.py
+++ b/solution.py
@@ -122,11 +122,8 @@
               (0, once0, half), (1, once0, half),
               None,
               (1, *twice))
-    order = range(n_twice - 1, -1, -1)
-
-    def ordered(p):
-        return n_twice - 1 - p
-
+    def ordered(p, n, swapped):
+        return jnp.where(swapped & (p < 2), n - 2 + p, n - 1 - p)
 
     def shares(k, c):
         if chunks[k] is None:
@@ -168,19 +165,25 @@
 
     def given(k, j):
         c = shares(k, col)
-        return remote(c, c, pan_send.at[k], pan_recv.at[k], row, (right, left, far, partner)[j])
+        return remote(c, c, pan_send.at[1 if chunks[k] is None else 0], pan_recv.at[k], row, (right, left, far, partner)[j])
 
     def across(k, j, c_):
         c = shares(k, (x_left, x_right, x_far)[j] * 2 + c_)
-        return remote(c, c, rel_send.at[k], pan_recv.at[k], row, partner)
-
-    def amount(k, n, send_sem):
+        return remote(c, c, rel_send.at[1 if chunks[k] is None else 0], pan_recv.at[k], row, partner)
+
+    def arrived(k):
+        n = 2 * n_x - 1
         if chunks[k] is None:
             c = epan.at[:, pl.ds(0, n)]
         else:
             d, l0, m = chunks[k]
             c = pan.at[d, pl.ds(l0, m), pl.ds(0, n)]
-        return remote(c, c, send_sem.at[k], pan_recv.at[k], row, partner)
+        return remote(c, c, pan_send.at[0], pan_recv.at[k], row, partner)
+
+    def departed(n, send_sem):
+        own, other = pan.at[:, :, pl.ds(0, n)], epan.at[:, pl.ds(0, n)]
+        remote(own, own, send_sem.at[0], pan_recv.at[0], row, partner).wait_send()
+        remote(other, other, send_sem.at[1], pan_recv.at[0], row, partner).wait_send()
 
     arrivals = [(j, c_) for j in range(3) for c_ in (1, 0)]
 
@@ -199,14 +202,14 @@
     def pass_on(k):
         @pl.when(core == 1)
         def _():
-            amount(k, 2 * n_x - 1, pan_send).wait_recv()
+            arrived(k).wait_recv()
             for j, c_ in arrivals:
                 across(k, j, c_).start()
 
     def settle(k):
         @pl.when(core == 0)
         def _():
-            amount(k, 2 * n_x - 1, pan_send).wait_recv()
+            arrived(k).wait_recv()
 
     def factor_chunks(*ks):
         with_above = any(chunks[k] is None for k in ks)
@@ -242,7 +245,8 @@
     panels_in.wait()
     give(0)
     tiles_in.wait()
-    for i in order:
+    for p in range(n_once):
+        i = ordered(p, n_once, first)
         upward(0, xin.at[once0 + i + shift], u1, i).start()
     for k in (1, 2, 3):
         give(k)
@@ -262,7 +266,7 @@
     pass_on(2)
 
     def early(p, carry):
-        i = ordered(p)
+        i = ordered(p, n_twice, last)
         upward(0, u1.at[i], u1, i).wait_recv()
         upper, lower = apply(0, twice0 + i, xin[twice0 + i], u1[i])
         xb[i] = upper
@@ -293,14 +297,8 @@
     pass_on(5)
     pass_on(6)
 
-    @pl.when(first)
-    def _():
-        downward(0, d1.at[n_once - 1], d1, n_once - 1).wait_recv()
-        xz[...] = jnp.where(flags[0, twice0] >= 0, xb[0], d1[n_once - 1])
-        upward(2, xz, u2, n_once - 1).start()
-
     def middle(p, carry):
-        i = ordered(p)
+        i = n_once - 1 - p
         l = once0 + i
         closed = last & (i == n_once - 1)
 
@@ -345,20 +343,26 @@
 
         return carry
 
-    lax.fori_loop(0, n_once - half, middle, 0)
-
+    lax.fori_loop(0, 1, middle, 0)
     settle(4)
     settle(5)
     settle(6)
     twin_flags.wait_recv()
     factor_chunks(4, 5, 6)
     pass_on(7)
-    lax.fori_loop(n_once - half, n_once, middle, 0)
+    @pl.when(first)
+    def _():
+        downward(0, d1.at[n_once - 1], d1, n_once - 1).wait_recv()
+        xz[...] = jnp.where(flags[0, twice0] >= 0, xb[0], d1[n_once - 1])
+        upward(2, xz, u2, n_once - 1).start()
+
+    lax.fori_loop(1, n_once, middle, 0)
+
     settle(7)
     factor_chunks(7)
 
     def late(p, carry):
-        i = ordered(p)
+        i = ordered(p, n_twice, last)
 
         @pl.when(jnp.logical_not(first & (i == 0)))
         def _():
@@ -421,22 +425,11 @@
     twin_flags.wait_send()
     for e in range(both):
         twin_tile(e).wait_send()
-    for k in range(len(chunks)):
-        amount(k, n_x, pan_send).wait_send()
-
-        @pl.when(core == 1)
-        def _():
-            amount(k, 2 * n_x - 2, rel_send).wait_send()
-
-    def close(i, carry):
-        @pl.when(jnp.logical_not(first & (i == 0)))
-        def _():
-            j = i - shift
-            remote(s2.at[j], out.at[once0 + i, 0], dn_send.at[2], dn_recv.at[2, j], below, col).wait_recv()
-
-        return carry
-
-    lax.fori_loop(0, n_once, close, 0)
+    departed(n_x, pan_send)
+
+    @pl.when(core == 1)
+    def _():
+        departed(2 * n_x - 2, rel_send)
 
     @pl.when(first)
     def _():
@@ -445,10 +438,24 @@
         remote(xz, d2, dn_send.at[2], dn_recv.at[2, n_once - 1], below, col).wait_recv()
         xb[0] = jnp.where(flags[1, twice0] >= 0, xf[0], d2[...])
         pltpu.make_async_copy(xb.at[0], out.at[twice0, 0], out_sem.at[0]).start()
-        own.wait()
+
+    def close(i, carry):
+        @pl.when(jnp.logical_not(first & (i == 0)))
+        def _():
+            j = i - shift
+            remote(s2.at[j], out.at[once0 + i, 0], dn_send.at[2], dn_recv.at[2, j], below, col).wait_recv()
+
+        return carry
+
+    lax.fori_loop(0, n_once, close, 0)
 
     left_down(2, n_twice)
-    pltpu.make_async_copy(xf, out.at[pl.ds(twice0, n_twice), 0], out_sem.at[0]).wait()
+
+    @pl.when(first)
+    def _():
+        pltpu.make_async_copy(xs.at[0], out.at[once0, 0], out_sem.at[1]).wait()
+
+    pltpu.make_async_copy(xf.at[pl.ds(0, n_twice)], out.at[pl.ds(twice0, n_twice), 0], out_sem.at[0]).wait()
 
 
 def local(n_row, n_x, eigvec, reflectors, sweep_group):
@@ -479,7 +486,7 @@
             pltpu.VMEM((pair, 2, band, band), bf16),
             pltpu.VMEM((pair, 2, band, 2 * band), bf16),
             dma, dma((2,)), dma((2,)), dma((pair,)), dma((pair,)),
-            dma, dma, dma((8,)), dma((8,)), dma((8,)),
+            dma, dma, dma((2,)), dma((8,)), dma((2,)),
             dma((3,)), dma((3, cap)), dma((3,)), dma((3, cap)), dma((2,)),
         ],
         compiler_params=pltpu.CompilerParams(

time: 52.4 us -> 52.3 us (level)
  the two profiles are of different devices: /device:TPU:1 before, /device:TPU:2 now
where the time goes in v7:
time: 52.3 us; the launch traced here: 52.2 us
  Pallas kernels  51.3 us (98%)
  local copies, waits for them, and re-layouts  0.97 us (2%)
    pallas_call x1, Pallas kernels, local(): pl.pallas_call(functools.partial(kernel, n_row, n_x, FEWER), out_shape=ja...  51.3 us

profile of v7, /device:TPU:2, one launch (start us, length us, event | category | flops | bytes accessed | tf_op | source)
XLA Modules:
  0.0 52.2 jit_solution(1847733224716630685)
XLA Ops:
  0.0 51.3 %shard_map.37 = f32[8,1,128,256]{3,2,1,0:T(8,128)S(1)} custom-call(f32[8,1,128,256]{3,2,1,0:T(8,128)} %refs_0_.1, f32[2,8,1,32,128]{4,3,2,1,0:T(8,128)} %refs_1_.1, s32[2,8]{1,0:T(2,128)} %bitcast.1), custom_call_target="tpu_custom_call" | custom-call | tf_op jit(solution)/shard_map/pallas_call | solution.py:471
  51.3 1.0 %copy.5 = f32[8,1,128,256]{3,2,1,0:T(8,128)} copy(f32[8,1,128,256]{3,2,1,0:T(8,128)S(1)} %shard_map.37) | data formatting | bytes 2097152

commit v8 on v7

--- a/solution.py
+++ b/solution.py
@@ -131,22 +131,22 @@
         d, l0, n = chunks[k]
         return pan.at[d, pl.ds(l0, n), c]
 
+    barrier = pltpu.get_barrier_semaphore()
+    for r_, c_ in ((below, col), (above, col), (row, partner)):
+        pl.semaphore_signal(barrier, inc=1, device_id=(r_, c_), device_id_type=MESH)
+
+    @pl.when(core == 1)
+    def _():
+        for x_ in (x_right, x_left, x_far):
+            for c_ in range(2):
+                pl.semaphore_signal(barrier, inc=1, device_id=(row, x_ * 2 + c_), device_id_type=MESH)
+
     tiles_in = pltpu.make_async_copy(eig.at[:, 0], xin, in_sem)
     tiles_in.start()
     panels_in = pltpu.make_async_copy(refl.at[:, :, 0], pan.at[:, :, col], pan_in)
     panels_in.start()
     flags_copy = pltpu.make_async_copy(flags_in, flags, flag_sem)
     flags_copy.start()
-
-    barrier = pltpu.get_barrier_semaphore()
-    for r_, c_ in ((above, col), (below, col), (row, partner)):
-        pl.semaphore_signal(barrier, inc=1, device_id=(r_, c_), device_id_type=MESH)
-
-    @pl.when(core == 1)
-    def _():
-        for x_ in (x_right, x_left, x_far):
-            for c_ in range(2):
-                pl.semaphore_signal(barrier, inc=1, device_id=(row, x_ * 2 + c_), device_id_type=MESH)
 
     pl.semaphore_wait(barrier, 6)
 
@@ -242,12 +242,12 @@
         active = flags[d, l] >= 0
         return (jnp.where(active, upper - change[:band], upper), jnp.where(active, lower - change[band:], lower))
 
-    panels_in.wait()
-    give(0)
     tiles_in.wait()
     for p in range(n_once):
         i = ordered(p, n_once, first)
         upward(0, xin.at[once0 + i + shift], u1, i).start()
+    panels_in.wait()
+    give(0)
     for k in (1, 2, 3):
         give(k)
     twin_panels.start()

time: 52.3 us -> 52.3 us (level)
  the two profiles are of different devices: /device:TPU:2 before, /device:TPU:4 now
where the time goes in v8:
time: 52.3 us; the launch traced here: 52.2 us
  Pallas kernels  51.3 us (98%)
  local copies, waits for them, and re-layouts  0.97 us (2%)
    pallas_call x1, Pallas kernels, local(): pl.pallas_call(functools.partial(kernel, n_row, n_x, FEWER), out_shape=ja...  51.3 us

profile of v8, /device:TPU:4, one launch (start us, length us, event | category | flops | bytes accessed | tf_op | source)
XLA Modules:
  0.0 52.2 jit_solution(849121428425585149)
XLA Ops:
  0.0 51.3 %shard_map.37 = f32[8,1,128,256]{3,2,1,0:T(8,128)S(1)} custom-call(f32[8,1,128,256]{3,2,1,0:T(8,128)} %refs_0_.1, f32[2,8,1,32,128]{4,3,2,1,0:T(8,128)} %refs_1_.1, s32[2,8]{1,0:T(2,128)} %bitcast.1), custom_call_target="tpu_custom_call" | custom-call | tf_op jit(solution)/shard_map/pallas_call | solution.py:471
  51.3 1.0 %copy.5 = f32[8,1,128,256]{3,2,1,0:T(8,128)} copy(f32[8,1,128,256]{3,2,1,0:T(8,128)S(1)} %shard_map.37) | data formatting | bytes 2097152

commit v9 on v8

--- a/solution.py
+++ b/solution.py
@@ -343,7 +343,8 @@
 
         return carry
 
-    lax.fori_loop(0, 1, middle, 0)
+    ahead = jnp.where(last, 2, 1)
+    lax.fori_loop(0, ahead, middle, 0)
     settle(4)
     settle(5)
     settle(6)
@@ -356,7 +357,7 @@
         xz[...] = jnp.where(flags[0, twice0] >= 0, xb[0], d1[n_once - 1])
         upward(2, xz, u2, n_once - 1).start()
 
-    lax.fori_loop(1, n_once, middle, 0)
+    lax.fori_loop(ahead, n_once, middle, 0)
 
     settle(7)
     factor_chunks(7)

time: 52.3 us -> 52 us (level)
  the two profiles are of different devices: /device:TPU:4 before, /device:TPU:2 now
where the time goes in v9:
time: 52 us; the launch traced here: 51.9 us
  Pallas kernels  51 us (98%)
  local copies, waits for them, and re-layouts  0.97 us (2%)
    pallas_call x1, Pallas kernels, local(): pl.pallas_call(functools.partial(kernel, n_row, n_x, FEWER), out_shape=ja...  51 us

profile of v9, /device:TPU:2, one launch (start us, length us, event | category | flops | bytes accessed | tf_op | source)
XLA Modules:
  0.0 51.9 jit_solution(12614383820619644924)
XLA Ops:
  0.0 51.0 %shard_map.37 = f32[8,1,128,256]{3,2,1,0:T(8,128)S(1)} custom-call(f32[8,1,128,256]{3,2,1,0:T(8,128)} %refs_0_.1, f32[2,8,1,32,128]{4,3,2,1,0:T(8,128)} %refs_1_.1, s32[2,8]{1,0:T(2,128)} %bitcast.1), custom_call_target="tpu_custom_call" | custom-call | tf_op jit(solution)/shard_map/pallas_call | solution.py:472
  51.0 1.0 %copy.5 = f32[8,1,128,256]{3,2,1,0:T(8,128)} copy(f32[8,1,128,256]{3,2,1,0:T(8,128)S(1)} %shard_map.37) | data formatting | bytes 2097152
